TPU v7x, 32 devices: a whole 2x2x4 slice. The times are simulated.
32 devices in a mesh: lon: 2 (over x), lat: 4 (over y, core), mem: 4 (over z).
Axes of the slice: x: 2, y: 2, z: 4, core: 2. Of those that a mesh axis runs over, the one named last changes fastest.
Arguments:
- anomalies: bfloat16 [32, 4, 128, 512], P('mem', None, 'lon', 'lat'), may hold values from -6 to 6
- spread: float32 [4, 128, 512], P(None, 'lon', 'lat'), may hold values from 0.5 to 2
- obs_index: int32 [2, 4, 2048], P('lon', 'lat'), may hold values from 0 to 32767
- innovation: float32 [2, 4, 2048], P('lon', 'lat'), may hold values from -6 to 6
- obs_weight: float32 [2, 4, 2048], P('lon', 'lat'), may hold values from 0.5 to 8
- band_width: int32 [2, 4], replicated, may hold values from 6 to 12, as said below
Outputs:
- control_ens: float32 [32, 4, 128, 512], P('mem', None, 'lon', 'lat')
- control_static: float32 [4, 128, 512], P(None, 'lon', 'lat')
Inputs may be any that keep to these rules, and one draw needn't show every extreme that they name: `obs_index`: A cell of the tile's 4 x 64 x 128 block, flattened with latitude fastest. `band_width`: in each of the two rows some level has exactly 12.
All inputs are finite; a program needn't handle non-finite values.
Results may differ from a plain program's by a relative error of at most 0.0003.
Values may be sent and summed in bfloat16 or wider, within the bound.
A program may use at most 64 MiB of HBM per device.

v0:
```python
import functools
import math

import jax
import jax.numpy as jnp
from jax import lax
from jax.experimental import pallas as pl
from jax.experimental.pallas import tpu as pltpu
from jax.sharding import PartitionSpec as P

BAND = 12
RIM = 2 * BAND

hybrid_ens = 0.75
hybrid_static = 0.25

MESH = pl.DeviceIdType.MESH
VMEM = pl.BlockSpec(memory_space=pltpu.VMEM)
F32 = jnp.float32
BF16 = jnp.bfloat16


def split2(x):
    hi = x.astype(BF16)
    return hi, (x - hi.astype(F32)).astype(BF16)


def dot3(left, right):
    lh, ll = left
    rh, rl = right
    d = functools.partial(jnp.dot, preferred_element_type=F32)
    return d(lh, rh) + (d(ll, rh) + d(lh, rl))


AXES = ("lon", "lat", "mem")


def fused(a_ref, s_ref, i_ref, w_ref, v_ref, bw_ref, ens_ref, static_ref, *scratch, dims):
    members, levels, lon_cells, lat_cells, sizes = dims
    (fc, fr, bc, br, qc, qr, send_al, send_ah, recv_al, recv_ah, pack_l, pack_h, recv_pl, recv_ph,
     fpack, xrh, xrl, two_c, two_r, two_l, one_c, one_r, one_l, bflat, dflat, cov, part,
     slots, slots2, dslots, dsend, smoothed_lat, send, recv, csend, crecv, dsems, drems) = scratch
    lon_n, lat_n, mem_n = sizes
    total = lon_n * lat_n * mem_n
    fields = members + 1
    ext = lon_cells + 2 * RIM
    rows = levels * lon_cells
    chunk = rows // mem_n
    coef_ens = math.sqrt(hybrid_ens / (members * mem_n))
    coef_static = math.sqrt(hybrid_static)
    mine = [lax.axis_index(a) for a in AXES]
    lat_at, me = mine[1], mine[2]
    has_low, has_high = lat_at > 0, lat_at < lat_n - 1

    def shifted(step):
        parts, rest = [], step
        for size in reversed(sizes):
            parts.append(rest % size)
            rest //= size
        return tuple(lax.rem(m + s, size) for m, s, size in zip(mine, reversed(parts), sizes))

    barrier = pltpu.get_barrier_semaphore()
    for step in range(1, total):
        pl.semaphore_signal(barrier, inc=1, device_id=shifted(step), device_id_type=MESH)

    used = [0]

    def remote(src, dst, where):
        k = used[0]
        used[0] += 1
        return pltpu.make_async_remote_copy(
            src_ref=src, dst_ref=dst, send_sem=send.at[k], recv_sem=recv.at[k],
            device_id=where, device_id_type=MESH,
        )

    lon_low = {"lon": lax.rem(mine[0] + lon_n - 1, lon_n)}
    lon_high = {"lon": lax.rem(mine[0] + 1, lon_n)}
    lat_low = {"lat": lax.rem(lat_at + lat_n - 1, lat_n)}
    lat_high = {"lat": lax.rem(lat_at + 1, lat_n)}
    own = pl.ds(0, lon_cells)
    rim = pl.ds(lon_cells, 2 * RIM)
    low_rows = pl.ds(lon_cells, RIM)
    high_rows = pl.ds(lon_cells + RIM, RIM)
    first_rows = pl.ds(0, RIM)
    last_rows = pl.ds(lon_cells - RIM, RIM)
    low_lanes = pl.ds(0, lat_cells)
    high_lanes = pl.ds(lat_cells, lat_cells)

    def lon_start(copies):
        for c in copies:
            c.start()

    def lon_wait(copies):
        for c in copies:
            c.wait()

    class Lat:
        def __init__(self, low_src, high_src, from_low, from_high):
            self.to_low = remote(low_src, from_high, lat_low)
            self.to_high = remote(high_src, from_low, lat_high)

        def start(self):
            pl.when(has_low)(self.to_low.start)
            pl.when(has_high)(self.to_high.start)

        def wait(self):
            pl.when(has_low)(self.to_low.wait_send)
            pl.when(has_high)(self.to_high.wait_send)
            pl.when(has_high)(self.to_low.wait_recv)
            pl.when(has_low)(self.to_high.wait_recv)

    def lane_pack(read, count):
        lane = lax.broadcasted_iota(jnp.int32, (count, lat_cells), 1)
        low = jnp.zeros((count, lat_cells), F32)
        high = low
        for l in range(levels):
            x = read(l)
            here = (lane >= l * RIM) & (lane < (l + 1) * RIM)
            low = jnp.where(here, pltpu.roll(x, (l * RIM) % lat_cells, 1), low)
            high = jnp.where(here, pltpu.roll(x, ((l + 1) * RIM) % lat_cells, 1), high)
        return low, high

    def zero_edges(ref, lead=()):
        @pl.when(jnp.logical_not(has_low))
        def _():
            ref[(*lead, slice(None), low_lanes)] = jnp.zeros((ext, lat_cells), F32)

        @pl.when(jnp.logical_not(has_high))
        def _():
            ref[(*lead, slice(None), high_lanes)] = jnp.zeros((ext, lat_cells), F32)

    def load_member(m, _):
        lows, highs = [], []
        for l in range(levels):
            x = a_ref[m, l].astype(F32)
            fc[l, m, :lon_cells, :] = x
            lows.append(x[:RIM])
            highs.append(x[lon_cells - RIM :])
        send_al[m] = jnp.concatenate(lows, axis=0).astype(BF16)
        send_ah[m] = jnp.concatenate(highs, axis=0).astype(BF16)
        return 0

    lax.fori_loop(0, members, load_member, 0)
    for l in range(levels):
        fc[l, members, :lon_cells, :] = s_ref[l]

    def pack_member(span, count):
        def go(m, _):
            low, high = lane_pack(lambda l: fc[l, m, span, :], count)
            pack_l[m, span, :] = low.astype(BF16)
            pack_h[m, span, :] = high.astype(BF16)
            return 0

        lax.fori_loop(0, members, go, 0)

    def lon_field(ref, lead):
        at = lambda span: ref.at[(slice(None), *lead, span, slice(None))]
        return [
            remote(at(first_rows), at(high_rows), lon_low),
            remote(at(last_rows), at(low_rows), lon_high),
        ]

    def lat_field(slot, dst, lead, span):
        at = lambda lanes: dst.at[(*lead, span, lanes)]
        return Lat(
            fpack.at[slot, 0, span, :], fpack.at[slot, 1, span, :], at(low_lanes), at(high_lanes)
        )

    def fill_pack(slot, read, span, count):
        low, high = lane_pack(lambda l: read(l, span), count)
        fpack[slot, 0, span, :] = low
        fpack[slot, 1, span, :] = high

    read_s = lambda l, span: fc[l, members, span, :]
    read_b = lambda l, span: bc[l, span, :]
    read_q = lambda l, span: qc[l, span, :]

    pl.semaphore_wait(barrier, total - 1)
    lon_a = [remote(send_al, recv_ah, lon_low), remote(send_ah, recv_al, lon_high)]
    lon_start(lon_a)
    lon_s = lon_field(fc, (members,))
    lon_start(lon_s)
    pack_member(own, lon_cells)
    lat_a = Lat(pack_l.at[:, own, :], pack_h.at[:, own, :], recv_pl.at[:, own, :], recv_ph.at[:, own, :])
    lat_a.start()

    idx, val_w = i_ref[...], w_ref[...]
    n_obs = idx.shape[1]
    row, lane = idx // lat_cells, idx % lat_cells
    at_row = (lax.broadcasted_iota(jnp.int32, (rows, n_obs), 0) == row).astype(F32).astype(BF16)
    at_lane = lax.broadcasted_iota(jnp.int32, (lat_cells, n_obs), 0) == lane
    for val, out in ((val_w, dflat), (val_w * v_ref[...], bflat)):
        acc = None
        for _ in range(3):
            piece_val = val.astype(BF16).astype(F32)
            val = val - piece_val
            placed = jnp.where(at_lane, piece_val, 0.0).astype(BF16)
            term = lax.dot_general(
                at_row, placed, (((1,), (1,)), ((), ())), preferred_element_type=F32
            )
            acc = term if acc is None else acc + term
        out[...] = acc
    for l in range(levels):
        bc[l, :lon_cells, :] = bflat[l * lon_cells : (l + 1) * lon_cells, :]
    lon_b = lon_field(bc, ())
    lon_start(lon_b)
    fill_pack(0, read_s, own, lon_cells)
    fill_pack(1, read_b, own, lon_cells)
    lat_sb = [lat_field(0, fr, (members,), own), lat_field(1, br, (), own)]
    for c in lat_sb:
        c.start()
    zero_edges(fr, (members,))
    zero_edges(br)
    zero_edges(qr)

    def iota(shape, dim):
        return lax.broadcasted_iota(jnp.int32, shape, dim)

    def ext_place(index, cells):
        return jnp.where(index < cells, index, jnp.where(index < cells + RIM, index - cells - RIM, index - RIM))

    def make_matrices(l, _):
        taps = (iota((8, 128), 1) - BAND).astype(F32)

        def weights(kind):
            width = bw_ref[kind, l].astype(F32) + jnp.zeros((1, 1), F32)

            def raw(o):
                return jnp.where(jnp.abs(o) <= width, jnp.exp(-0.5 * (o / (0.5 * width)) ** 2), 0.0)

            norm = jnp.sum(raw(taps)[:1], axis=1, keepdims=True)
            return lambda o: raw(o.astype(F32)) / norm

        def put(ref, where, value):
            hi, lo = split2(value)
            ref[(0, *where)] = hi
            ref[(1, *where)] = lo

        w = weights(0)
        mids = 128 * pl.cdiv(lon_cells + 2 * BAND, 128)
        near = w(iota((lon_cells, mids), 0) - (iota((lon_cells, mids), 1) - BAND))
        near = jnp.where(iota((lon_cells, mids), 1) < lon_cells + 2 * BAND, near, 0.0)
        far = w(iota((mids, ext), 0) - BAND - ext_place(iota((mids, ext), 1), lon_cells))
        put(two_l, (l,), dot3(split2(near), split2(far)))
        put(one_l, (l,), w(iota((lon_cells, ext), 0) - ext_place(iota((lon_cells, ext), 1), lon_cells)))

        w = weights(1)
        mids = 128 * pl.cdiv(lat_cells + 2 * BAND, 128)
        mid = iota((mids, lat_cells), 0) - BAND
        place = lat_at * lat_cells + mid
        keep = (place >= 0) & (place < lat_cells * lat_n) & (mid < lat_cells + BAND)
        back = split2(jnp.where(keep, w(mid - iota((mids, lat_cells), 1)), 0.0))
        out = iota((lat_cells, lat_cells), 1)
        here = iota((lat_cells, mids), 0) - (iota((lat_cells, mids), 1) - BAND)
        put(two_c, (l,), dot3(split2(w(here)), back))
        put(one_c, (l,), w(iota((lat_cells, lat_cells), 0) - out))
        columns = pl.ds(pl.multiple_of(l * lat_cells, lat_cells), lat_cells)
        for side in range(2):
            shift = -RIM if side == 0 else lat_cells
            span = pl.ds(side * lat_cells, lat_cells)

            def rim_at(shape):
                p = iota(shape, 0) - l * RIM
                return p + shift, (p >= 0) & (p < RIM)

            pos, ok = rim_at((lat_cells, mids))
            there = jnp.where(ok, w(pos - (iota((lat_cells, mids), 1) - BAND)), 0.0)
            put(two_r, (span, columns), dot3(split2(there), back))
            pos, ok = rim_at((lat_cells, lat_cells))
            put(one_r, (span, columns), jnp.where(ok, w(pos - out), 0.0))
        return 0

    lax.fori_loop(0, levels, make_matrices, 0)

    def lat_part(yc, yr, c_mat, r_mat, l, span, count):
        columns = pl.ds(pl.multiple_of(l * lat_cells, lat_cells), lat_cells)
        xc = split2((fc[l, :, span, :] * yc[l, span, :][None]).reshape(fields * count, lat_cells))
        xr = (
            xrh[:, span, :].reshape(fields * count, 2 * lat_cells),
            xrl[:, span, :].reshape(fields * count, 2 * lat_cells),
        )
        t = dot3(xc, (c_mat[0, l], c_mat[1, l]))
        t = t + dot3(xr, (r_mat[0, :, columns], r_mat[1, :, columns]))
        for h, half in enumerate(split2(t)):
            smoothed_lat[h, l, span, :] = jnp.concatenate(
                [half[f * count : (f + 1) * count] for f in range(fields)], axis=1
            )

    def rim_products(yr, span):
        def go(f, _):
            hi, lo = split2(fr[f, span, :] * yr[span, :])
            xrh[f, span, :], xrl[f, span, :] = hi, lo
            return 0

        lax.fori_loop(0, fields, go, 0)

    def apply_own(yc, yr, mats):
        rim_products(yr, own)

        def go(l, _):
            lat_part(yc, yr, mats[0], mats[1], l, own, lon_cells)
            return 0

        lax.fori_loop(0, levels, go, 0)

    def apply_rim(yc, yr, mats, finish):
        rim_products(yr, rim)

        def go(i, _):
            l = lax.rem(me + 1 + i, levels)
            lat_part(yc, yr, mats[0], mats[1], l, rim, 2 * RIM)
            u = dot3((mats[2][0, l], mats[2][1, l]), (smoothed_lat[0, l], smoothed_lat[1, l]))
            finish(i, l, [u[:, f * lat_cells : (f + 1) * lat_cells] for f in range(fields)])
            return 0

        lax.fori_loop(0, levels, go, 0)

    def unpack_lat(span, count):
        for ref, keep, lanes in ((recv_pl, has_low, low_lanes), (recv_ph, has_high, high_lanes)):
            def go(m, _):
                fr[m, span, lanes] = ref[m, span, :].astype(F32)
                return 0

            def clear(m, _):
                fr[m, span, lanes] = jnp.zeros((count, lat_cells), F32)
                return 0

            @pl.when(keep)
            def _():
                lax.fori_loop(0, members, go, 0)

            @pl.when(jnp.logical_not(keep))
            def _():
                lax.fori_loop(0, members, clear, 0)

    lat_a.wait()
    unpack_lat(own, lon_cells)
    for c in lat_sb:
        c.wait()
    apply_own(bc, br, (two_c, two_r, two_l))

    lon_wait(lon_a)

    def unpack_member(m, _):
        low, high = recv_al[m].astype(F32), recv_ah[m].astype(F32)
        for l in range(levels):
            fc[l, m, low_rows, :] = low[l * RIM : (l + 1) * RIM]
            fc[l, m, high_rows, :] = high[l * RIM : (l + 1) * RIM]
        return 0

    lax.fori_loop(0, members, unpack_member, 0)
    pack_member(rim, 2 * RIM)
    lat_a2 = Lat(pack_l.at[:, rim, :], pack_h.at[:, rim, :], recv_pl.at[:, rim, :], recv_ph.at[:, rim, :])
    lat_a2.start()
    lon_wait(lon_s)
    lon_wait(lon_b)
    fill_pack(0, read_s, rim, 2 * RIM)
    fill_pack(1, read_b, rim, 2 * RIM)
    lat_sb2 = [lat_field(0, fr, (members,), rim), lat_field(1, br, (), rim)]
    for c in lat_sb2:
        c.start()
    lat_a2.wait()
    unpack_lat(rim, 2 * RIM)
    for c in lat_sb2:
        c.wait()

    def piece(owner):
        return pl.ds(pl.multiple_of(owner * chunk, chunk), chunk)

    def mem_copy(src, dst, j, group):
        return pltpu.make_async_remote_copy(
            src_ref=src, dst_ref=dst, send_sem=csend.at[group, j], recv_sem=crecv.at[group, j],
            device_id={"mem": lax.rem(me + j, mem_n)}, device_id_type=MESH,
        )

    def sum_copy(dst, j, group):
        return mem_copy(part.at[piece(lax.rem(me + j, mem_n))], dst.at[j], j, group)

    by_level = levels == mem_n

    def finish_cov(dst, group):
        def finish(i, l, smoothed):
            acc = fc[l, 0, :lon_cells, :] * smoothed[0]
            for f in range(1, members):
                acc = acc + fc[l, f, :lon_cells, :] * smoothed[f]
            acc = acc * (coef_ens * coef_ens)
            acc = acc + fc[l, members, :lon_cells, :] * smoothed[members] * (coef_static**2 / mem_n)
            part[pl.ds(pl.multiple_of(l * lon_cells, lon_cells), lon_cells), :] = acc
            if by_level:
                @pl.when(i < mem_n - 1)
                def _():
                    sum_copy(dst, i + 1, group).start()

        return finish

    def scatter_sum(dst, group):
        copies = [sum_copy(dst, j, group) for j in range(1, mem_n)]
        if not by_level:
            for copy in copies:
                copy.start()
        acc = part[piece(me), :]
        for j, copy in enumerate(copies):
            copy.wait_recv()
            acc = acc + dst[j + 1]
        for copy in copies:
            copy.wait_send()
        return acc

    def dots_start(left, right, group):
        at = iota((2, lat_cells), 0)
        a = jnp.sum(left, axis=0, keepdims=True)
        b = jnp.sum(right, axis=0, keepdims=True)
        dsend[group] = jnp.where(at == 0, a, b)
        copies = []
        for step in range(1, total):
            copy = pltpu.make_async_remote_copy(
                src_ref=dsend.at[group], dst_ref=dslots.at[group, step],
                send_sem=dsems.at[group, step], recv_sem=drems.at[group, step],
                device_id=shifted(step), device_id_type=MESH,
            )
            copy.start()
            copies.append(copy)
        return copies

    def dots_end(copies, group):
        for copy in copies:
            copy.wait()
        block = dsend[group] + jnp.sum(dslots[group, 1:], axis=0)
        sums = jnp.sum(block, axis=1, keepdims=True)
        return sums[0:1], sums[1:2]

    two, one = (two_c, two_r, two_l), (one_c, one_r, one_l)
    apply_rim(bc, br, two, finish_cov(slots, 0))
    acc = scatter_sum(slots, 0)
    cov[piece(me), :] = acc
    back = [mem_copy(cov.at[piece(me)], cov.at[piece(me)], j, 1) for j in range(1, mem_n)]
    for copy in back:
        copy.start()
    rhs_mine, diag_mine, cov_mine = bflat[piece(me), :], dflat[piece(me), :], acc
    image_mine = rhs_mine + diag_mine * cov_mine
    dots0 = dots_start(rhs_mine * cov_mine, cov_mine * image_mine, 0)
    for copy in back:
        copy.wait()
    for l in range(levels):
        span = slice(l * lon_cells, (l + 1) * lon_cells)
        qc[l, :lon_cells, :] = bflat[span, :] + dflat[span, :] * cov[span, :]
    lon_q = lon_field(qc, ())
    lon_start(lon_q)
    fill_pack(2, read_q, own, lon_cells)
    lat_q = lat_field(2, qr, (), own)
    lat_q.start()
    lon_wait(lon_q)
    fill_pack(2, read_q, rim, 2 * RIM)
    lat_q2 = lat_field(2, qr, (), rim)
    lat_q2.start()
    lat_q.wait()

    apply_own(qc, qr, two)
    lat_q2.wait()
    apply_rim(qc, qr, two, finish_cov(slots2, 2))
    cov_q = scatter_sum(slots2, 2)
    norm0, curve0 = dots_end(dots0, 0)
    alpha0 = norm0 / curve0
    resid = rhs_mine - alpha0 * image_mine
    cov_r = cov_mine - alpha0 * cov_q
    norm1, curve1 = dots_end(dots_start(resid * cov_r, cov_r * (resid + diag_mine * cov_r), 1), 1)
    beta = norm1 / norm0
    alpha1 = norm1 / (curve1 - beta * norm1 / alpha0)

    def combine(b, q):
        return alpha0 * b + alpha1 * ((b - alpha0 * q) + beta * b)

    for l in range(levels):
        bc[l] = combine(bc[l], qc[l])
    br[...] = combine(br[...], qr[...])

    def finish_control(i, l, smoothed):
        for f in range(members):
            ens_ref[f, l] = coef_ens * smoothed[f]
        static_ref[l] = coef_static * smoothed[members]

    apply_own(bc, br, one)
    apply_rim(bc, br, one, finish_control)


def per_device(anomalies, spread, obs_index, innovation, obs_weight, band_width):
    members = anomalies.shape[0]
    levels, lon_cells, lat_cells = spread.shape
    sizes = tuple(lax.axis_size(a) for a in AXES)
    mem_n, total = sizes[2], math.prod(sizes)
    fields = members + 1
    ext = lon_cells + 2 * RIM
    rows = levels * lon_cells
    chunk = rows // mem_n
    v = pltpu.VMEM
    sem = pltpu.SemaphoreType.DMA
    edge = v((members, levels * RIM, lat_cells), BF16)
    packed = v((members, ext, lat_cells), BF16)
    field = v((levels, ext, lat_cells), F32)
    field_rim = v((ext, 2 * lat_cells), F32)
    mats = [
        v((2, levels, lat_cells, lat_cells), BF16),
        v((2, 2 * lat_cells, levels * lat_cells), BF16),
        v((2, levels, lon_cells, ext), BF16),
    ]
    flat = v((rows, lat_cells), F32)
    scratch = [
        v((levels, fields, ext, lat_cells), F32),
        v((fields, ext, 2 * lat_cells), F32),
        field, field_rim, field, field_rim,
        edge, edge, edge, edge,
        packed, packed, packed, packed,
        v((3, 2, ext, lat_cells), F32),
        v((fields, ext, 2 * lat_cells), BF16),
        v((fields, ext, 2 * lat_cells), BF16),
        *mats, *mats,
        flat, flat, flat, flat,
        v((mem_n, chunk, lat_cells), F32),
        v((mem_n, chunk, lat_cells), F32),
        v((2, total, 2, lat_cells), F32),
        v((2, 2, lat_cells), F32),
        v((2, levels, ext, fields * lat_cells), BF16),
        sem((32,)), sem((32,)), sem((3, mem_n)), sem((3, mem_n)), sem((2, total)), sem((2, total)),
    ]
    kernel = functools.partial(fused, dims=(members, levels, lon_cells, lat_cells, sizes))
    return pl.pallas_call(
        kernel,
        out_shape=[
            jax.ShapeDtypeStruct((members, levels, lon_cells, lat_cells), F32),
            jax.ShapeDtypeStruct((levels, lon_cells, lat_cells), F32),
        ],
        in_specs=[VMEM] * 5 + [pl.BlockSpec(memory_space=pltpu.SMEM)],
        out_specs=[VMEM] * 2,
        scratch_shapes=scratch,
        compiler_params=pltpu.CompilerParams(
            collective_id=0, has_side_effects=True, vmem_limit_bytes=60 * 2**20
        ),
    )(
        anomalies, spread, obs_index.reshape(1, -1), obs_weight.reshape(1, -1),
        innovation.reshape(1, -1), band_width,
    )


def solution(mesh):
    return jax.shard_map(
        per_device,
        mesh=mesh,
        in_specs=(
            P("mem", None, "lon", "lat"),
            P(None, "lon", "lat"),
            P("lon", "lat", None),
            P("lon", "lat", None),
            P("lon", "lat", None),
            P(),
        ),
        out_specs=(P("mem", None, "lon", "lat"), P(None, "lon", "lat")),
        check_vma=False,
    )
```

profile of v0, /device:TPU:0, one launch (start us, length us, event | category | flops | bytes accessed | tf_op | source)
XLA Modules:
  0.0 65.9 jit_solution(12518978149945424673)
XLA Ops:
  0.6 62.2 %shard_map.77 = (f32[8,4,64,128]{3,2,1,0:T(8,128)}, f32[4,64,128]{2,1,0:T(8,128)}) custom-call(bf16[8,4,64,128]{3,2,1,0:T(8,128)(2,1)} %a_ref.1, f32[4,64,128]{2,1,0:T(8,128)} %s_ref.1, s32[1,2048]{1,0:T(1,128)} %bitcast.3, f32[1,2048]{1,0:T(1,128)} %bitcast.4, f32[1,2048]{1,0:T(1,128)} %bitcast.5, s32[2,4]{1,0:T(2,128)} %bw_ref.1), custom_call_target="tpu_custom_call" | custom-call | tf_op jit(solution)/shard_map/pallas_call | solution.py:526
  62.9 0.0 copy-start
  62.9 2.3 %copy.10 = f32[8,4,64,128]{3,2,1,0:T(8,128)} copy(f32[8,4,64,128]{3,2,1,0:T(8,128)} %get-tuple-element.4) | data formatting | bytes 2097152
  65.2 0.0 copy-done
  65.2 0.7 copy.11
Async XLA Ops:
  62.9 2.4 %copy-start = (f32[4,64,128]{2,1,0:T(8,128)S(1)}, f32[4,64,128]{2,1,0:T(8,128)}, u32[]{:S(2)}) copy-start(f32[4,64,128]{2,1,0:T(8,128)} %get-tuple-element.5) | copy-start | bytes 393220
where the time goes:
time: 66.1 us; the launch traced here: 65.9 us
  Pallas kernels  62.2 us (94%)
  local copies, waits for them, and re-layouts  3 us (5%)
    pallas_call x1, Pallas kernels, per_device(): pl.pallas_call(kernel, out_shape=[jax.ShapeDtypeStruct((members, levels,...  62.2 us
    unnamed x4, local copies, waits for them, and re-layouts  3 us

commit v1 on v0

--- a/solution.py
+++ b/solution.py
@@ -541,9 +541,567 @@
     )
 
 
+def paired(a_ref, s_ref, i_ref, w_ref, v_ref, bw_ref, ub_ref, uq_ref, st_ref, coef_ref, *scratch, dims):
+    members, levels, lon_cells, lat_cells, sizes = dims
+    (acen, arim, plo, phi, scen, srim, spack, oidx, ow, ov, at_row, grid, grim, gpack, cov, orecv,
+     drecv, mat_c, mat_r, lon_t, lon_l, xr, ts, ubuf, stat, send, recv, done) = scratch
+    lon_n, lat_n, mem_n = sizes
+    half = members // lon_n
+    full = lon_n * lon_cells
+    group = lon_n * mem_n
+    rows = levels * lon_cells
+    wide = lat_cells
+    n_obs = i_ref.shape[1]
+    coef_ens = math.sqrt(hybrid_ens / (members * mem_n))
+    coef_static = math.sqrt(hybrid_static)
+    at_lon, lat_at, me = (lax.axis_index(a) for a in AXES)
+    other = 1 - at_lon
+    has_low, has_high = lat_at > 0, lat_at < lat_n - 1
+    my_id = at_lon * mem_n + me
+
+    def group_peer(step):
+        peer = lax.rem(my_id + step, group)
+        return {"lon": peer // mem_n, "mem": lax.rem(peer, mem_n)}
+
+    def lat_peer(step):
+        return {"lat": lax.rem(lat_at + step, lat_n)}
+
+    barrier = pltpu.get_barrier_semaphore()
+    for step in range(1, group):
+        pl.semaphore_signal(barrier, inc=1, device_id=group_peer(step), device_id_type=MESH)
+    for step in range(1, lat_n):
+        pl.semaphore_signal(barrier, inc=1, device_id=lat_peer(step), device_id_type=MESH)
+
+    used = [0]
+
+    def remote(src, dst, where):
+        k = used[0]
+        used[0] += 1
+        return pltpu.make_async_remote_copy(
+            src_ref=src, dst_ref=dst, send_sem=send.at[k], recv_sem=recv.at[k],
+            device_id=where, device_id_type=MESH,
+        )
+
+    partner = {"lon": other}
+    lat_low = {"lat": lax.rem(lat_at + lat_n - 1, lat_n)}
+    lat_high = {"lat": lax.rem(lat_at + 1, lat_n)}
+    own_rows = pl.ds(pl.multiple_of(at_lon * lon_cells, lon_cells), lon_cells)
+    far_rows = pl.ds(pl.multiple_of(other * lon_cells, lon_cells), lon_cells)
+    all_rows = pl.ds(0, full)
+    low_lanes = pl.ds(0, wide)
+    high_lanes = pl.ds(wide, wide)
+
+    class Lat:
+        def __init__(self, low_src, high_src, from_low, from_high):
+            self.to_low = remote(low_src, from_high, lat_low)
+            self.to_high = remote(high_src, from_low, lat_high)
+
+        def start(self):
+            pl.when(has_low)(self.to_low.start)
+            pl.when(has_high)(self.to_high.start)
+
+        def wait(self):
+            pl.when(has_low)(self.to_low.wait_send)
+            pl.when(has_high)(self.to_high.wait_send)
+            pl.when(has_high)(self.to_low.wait_recv)
+            pl.when(has_low)(self.to_high.wait_recv)
+
+    def iota(shape, dim):
+        return lax.broadcasted_iota(jnp.int32, shape, dim)
+
+    def lane_pack(read, count, at_levels=None):
+        lane = iota((count, wide), 1)
+        low = jnp.zeros((count, wide), F32)
+        high = low
+        for l in range(levels) if at_levels is None else at_levels:
+            x = read(l)
+            here = (lane >= l * RIM) & (lane < (l + 1) * RIM)
+            low = jnp.where(here, pltpu.roll(x, lax.rem(l * RIM, wide), 1), low)
+            high = jnp.where(here, pltpu.roll(x, lax.rem((l + 1) * RIM, wide), 1), high)
+        return low, high
+
+    def actual(p):
+        return lax.rem(at_lon * half + p, members)
+
+    def fill(p, _):
+        acen[p, :, own_rows, :] = a_ref[actual(p)]
+        return 0
+
+    def pack_member(p, span, count):
+        low, high = lane_pack(lambda l: acen[p, l, span, :].astype(F32), count)
+        plo[p, span, :] = low.astype(BF16)
+        phi[p, span, :] = high.astype(BF16)
+
+    def pack_static(span, count):
+        low, high = lane_pack(lambda l: scen[span, :], count, [me])
+        spack[0, span, :] = low
+        spack[1, span, :] = high
+
+    def lat_members(which, span):
+        return Lat(
+            plo.at[which, span, :], phi.at[which, span, :],
+            arim.at[which, span, low_lanes], arim.at[which, span, high_lanes],
+        )
+
+    def lat_static(span):
+        return Lat(
+            spack.at[0, span, :], spack.at[1, span, :],
+            srim.at[span, low_lanes], srim.at[span, high_lanes],
+        )
+
+    def lat_grid(g):
+        return Lat(gpack.at[g, 0], gpack.at[g, 1], grim.at[g, :, low_lanes], grim.at[g, :, high_lanes])
+
+    first, second = pl.ds(0, half), pl.ds(half, half)
+    x_obs = [
+        remote(src, dst.at[1], partner) for src, dst in ((i_ref, oidx), (w_ref, ow), (v_ref, ov))
+    ]
+    x_static = remote(s_ref.at[me], scen.at[own_rows], partner)
+    x_first = [
+        remote(a_ref.at[other * half + p], acen.at[p, :, own_rows, :], partner) for p in range(half)
+    ]
+    x_second = remote(
+        a_ref.at[pl.ds(at_lon * half, half)], acen.at[second, :, own_rows, :], partner
+    )
+    pl.semaphore_wait(barrier, group - 1 + lat_n - 1)
+    for copy in [*x_obs, x_static, *x_first]:
+        copy.start()
+
+    lax.fori_loop(0, members, fill, 0)
+
+    def pack_first(p, _):
+        pack_member(p, own_rows, lon_cells)
+        return 0
+
+    lax.fori_loop(0, half, pack_first, 0)
+    lat_a = lat_members(first, own_rows)
+    lat_a.start()
+    scen[own_rows, :] = s_ref[me]
+    pack_static(own_rows, lon_cells)
+    lat_s = lat_static(own_rows)
+    lat_s.start()
+
+    @pl.when(jnp.logical_not(has_low))
+    def _():
+        arim[:, :, low_lanes] = jnp.zeros((members, full, wide), BF16)
+        srim[:, low_lanes] = jnp.zeros((full, wide), F32)
+        grim[:, :, low_lanes] = jnp.zeros((2, full, wide), F32)
+
+    @pl.when(jnp.logical_not(has_high))
+    def _():
+        arim[:, :, high_lanes] = jnp.zeros((members, full, wide), BF16)
+        srim[:, high_lanes] = jnp.zeros((full, wide), F32)
+        grim[:, :, high_lanes] = jnp.zeros((2, full, wide), F32)
+
+    slot_rows = (own_rows, far_rows)
+    slot_tile = (at_lon, other)
+
+    def mark_rows(s):
+        row = oidx[s] // wide
+        at_row[s] = (iota((rows, n_obs), 0) == row).astype(F32).astype(BF16)
+
+    def scatter(s, value, g):
+        at_lane = iota((wide, n_obs), 0) == oidx[s] % wide
+        hi = value.astype(BF16).astype(F32)
+        lo = value - hi
+        placed = jnp.concatenate(
+            [jnp.where(at_lane, hi, 0.0).astype(BF16), jnp.where(at_lane, lo, 0.0).astype(BF16)], axis=0
+        )
+        out = lax.dot_general(
+            at_row[s], placed, (((1,), (1,)), ((), ())), preferred_element_type=F32
+        )
+        out = out[:, :wide] + out[:, wide:]
+        for l in range(levels):
+            grid[g, l, slot_rows[s], :] = out[l * lon_cells : (l + 1) * lon_cells]
+
+    def gather(s, g):
+        hi, lo = split2(cov[slot_tile[s]].T)
+        left = jnp.concatenate([hi, lo], axis=0)
+        step = 512 if n_obs % 512 == 0 else n_obs
+        for c in range(0, n_obs, step):
+            part = jnp.dot(left, at_row[s, :, c : c + step], preferred_element_type=F32)
+            lane = oidx[s, :, c : c + step] % wide
+            here = iota((wide, step), 0) == lane
+            value = jnp.where(here, part[:wide] + part[wide:], 0.0)
+            orecv[g, my_id, slot_tile[s], :, c : c + step] = jnp.sum(value, axis=0, keepdims=True)
+
+    def send_grid(g):
+        low, high = lane_pack(lambda l: grid[g, l], full)
+        gpack[g, 0] = low
+        gpack[g, 1] = high
+        copy = lat_grid(g)
+        copy.start()
+        return copy
+
+    oidx[0], ow[0], ov[0] = i_ref[...], w_ref[...], v_ref[...]
+    mark_rows(0)
+    scatter(0, ow[0] * ov[0], 0)
+
+    def make_matrices(l, _):
+        taps = (iota((8, 128), 1) - BAND).astype(F32)
+
+        def weights(kind):
+            width = bw_ref[kind, l].astype(F32) + jnp.zeros((1, 1), F32)
+
+            def raw(o):
+                return jnp.where(jnp.abs(o) <= width, jnp.exp(-0.5 * (o / (0.5 * width)) ** 2), 0.0)
+
+            norm = jnp.sum(raw(taps)[:1], axis=1, keepdims=True)
+            return lambda o: raw(o.astype(F32)) / norm
+
+        def put_lon(ref, count, value):
+            hi, lo = split2(value)
+            ref[l, :count, :full] = hi
+            ref[l, :count, full:] = hi
+            ref[l, count:, :full] = lo
+            ref[l, count:, full:] = jnp.zeros((count, full), BF16)
+
+        w = weights(0)
+
+        def ring(count, base):
+            d = iota((count, full), 1) - (iota((count, full), 0) + base)
+            d = jnp.where(d > full // 2, d - full, d)
+            return w(jnp.where(d < -(full // 2), d + full, d))
+
+        circle = split2(ring(full, 0))
+        put_lon(lon_t, full, dot3(circle, circle))
+        put_lon(lon_l, lon_cells, ring(lon_cells, at_lon * lon_cells))
+
+        def put_lat(ref, kind, hi_at, lo_at, value):
+            hi, lo = split2(value)
+            ref[kind, l, pl.ds(hi_at, wide), :wide] = hi
+            ref[kind, l, pl.ds(hi_at, wide), wide:] = lo
+            ref[kind, l, pl.ds(lo_at, wide), :wide] = hi
+            ref[kind, l, pl.ds(lo_at, wide), wide:] = jnp.zeros((wide, wide), BF16)
+
+        w = weights(1)
+        mids = 128 * pl.cdiv(wide + 2 * BAND, 128)
+        mid = iota((mids, wide), 0) - BAND
+        place = lat_at * wide + mid
+        keep = (place >= 0) & (place < wide * lat_n) & (mid < wide + BAND)
+        back = split2(jnp.where(keep, w(mid - iota((mids, wide), 1)), 0.0))
+        out = iota((wide, wide), 1)
+        here = iota((wide, mids), 0) - (iota((wide, mids), 1) - BAND)
+        put_lat(mat_c, 0, 0, wide, dot3(split2(w(here)), back))
+        put_lat(mat_c, 1, 0, wide, w(iota((wide, wide), 0) - out))
+        for side in range(2):
+            shift = -RIM if side == 0 else wide
+
+            def rim_at(shape):
+                p = iota(shape, 0) - l * RIM
+                return p + shift, (p >= 0) & (p < RIM)
+
+            pos, ok = rim_at((wide, mids))
+            there = jnp.where(ok, w(pos - (iota((wide, mids), 1) - BAND)), 0.0)
+            put_lat(mat_r, 0, side * wide, (2 + side) * wide, dot3(split2(there), back))
+            pos, ok = rim_at((wide, wide))
+            put_lat(mat_r, 1, side * wide, (2 + side) * wide, jnp.where(ok, w(pos - out), 0.0))
+        return 0
+
+    lax.fori_loop(0, levels, make_matrices, 0)
+
+    for copy in x_obs:
+        copy.wait()
+    mark_rows(1)
+    scatter(1, ow[1] * ov[1], 0)
+    lat_b = send_grid(0)
+
+    x_static.wait()
+    pack_static(far_rows, lon_cells)
+    lat_s2 = lat_static(far_rows)
+    lat_s2.start()
+    lat_a2 = []
+    for p in range(half):
+        x_first[p].wait()
+        pack_member(p, far_rows, lon_cells)
+        copy = lat_members(p, far_rows)
+        copy.start()
+        lat_a2.append(copy)
+
+    def dot(a, b):
+        return jnp.dot(a, b, preferred_element_type=F32)
+
+    def rim_split(x):
+        hi, lo = split2(x)
+        return jnp.concatenate([hi, lo], axis=1)
+
+    def rim_member(g, p):
+        xr[p] = rim_split(arim[p].astype(F32) * grim[g])
+
+    def along_lat(x, rims, kind, l):
+        t = dot(rim_split(x), mat_c[kind, l]) + dot(rims, mat_r[kind, l])
+        return split2(t[:, :wide] + t[:, wide:])
+
+    def lat_member(g, p, kind, l):
+        hi, lo = along_lat(acen[p, l].astype(F32) * grid[g, l], xr[p], kind, l)
+        ts[l, :full, p * wide : (p + 1) * wide] = hi
+        ts[l, full:, p * wide : (p + 1) * wide] = lo
+
+    def lat_own_static(g, kind):
+        rims = rim_split(srim[...] * grim[g])
+        hi, lo = along_lat(scen[...] * grid[g, me], rims, kind, me)
+        return jnp.concatenate([hi, lo], axis=0)
+
+    def cov_level(l):
+        u = dot(lon_t[l], ts[l, :, : half * wide])
+        u = u[:full] + u[full:]
+        acc = acen[0, l].astype(F32) * u[:, :wide]
+        for p in range(1, half):
+            acc = acc + acen[p, l].astype(F32) * u[:, p * wide : (p + 1) * wide]
+        acc = acc * (coef_ens * coef_ens)
+        at = pl.ds(pl.multiple_of(l * lon_cells, lon_cells), lon_cells)
+        for j in range(lon_n):
+            cov[j, at, :] = acc[j * lon_cells : (j + 1) * lon_cells]
+
+    def cov_static(g):
+        u = dot(lon_t[me], lat_own_static(g, 0))
+        acc = scen[...] * (u[:full] + u[full:]) * (coef_static**2 / lon_n)
+        at = pl.ds(pl.multiple_of(me * lon_cells, lon_cells), lon_cells)
+        for j in range(lon_n):
+            cov[j, at, :] = cov[j, at, :] + acc[j * lon_cells : (j + 1) * lon_cells]
+
+    def share(g):
+        for s in range(lon_n):
+            gather(s, g)
+        copies = []
+        for step in range(1, group):
+            copy = remote(orecv.at[g, my_id], orecv.at[g, my_id], group_peer(step))
+            copy.start()
+            copies.append(copy)
+        return copies
+
+    def shared(copies, g):
+        for copy in copies:
+            copy.wait()
+        sums = []
+        for s in range(lon_n):
+            acc = orecv[g, 0, slot_tile[s]]
+            for k in range(1, group):
+                acc = acc + orecv[g, k, slot_tile[s]]
+            sums.append(acc)
+        return sums
+
+    def out_level(g, p0, n):
+        def go(l, _):
+            for p in range(p0, p0 + n):
+                lat_member(g, p, 1, l)
+            u = dot(lon_l[l], ts[l, :, p0 * wide : (p0 + n) * wide])
+            u = (u[:lon_cells] + u[lon_cells:]) * coef_ens
+            for p in range(n):
+                ubuf[g, actual(p0 + p), l] = u[:, p * wide : (p + 1) * wide]
+            return 0
+
+        lax.fori_loop(0, levels, go, 0)
+
+    def rim_span(g, p0, n):
+        def go(p, _):
+            rim_member(g, p)
+            return 0
+
+        lax.fori_loop(p0, p0 + n, go, 0)
+
+    def out_static(g):
+        u = dot(lon_l[me], lat_own_static(g, 1))
+        stat[me, g] = (u[:lon_cells] + u[lon_cells:]) * coef_static
+        copies = []
+        for j in range(1, mem_n):
+            copy = remote(stat.at[me, g], stat.at[me, g], {"mem": lax.rem(me + j, mem_n)})
+            copy.start()
+            copies.append(copy)
+        return copies
+
+    def dots_start(g, left, right):
+        def total(pairs):
+            acc = None
+            for x in pairs:
+                for c in range(0, n_obs, 128):
+                    part = x[:, c : c + 128]
+                    acc = part if acc is None else acc + part
+            return acc
+
+        at = iota((2, 128), 0)
+        drecv[g, lat_at] = jnp.where(at == 0, total(left), total(right))
+        copies = []
+        for step in range(1, lat_n):
+            copy = remote(drecv.at[g, lat_at], drecv.at[g, lat_at], lat_peer(step))
+            copy.start()
+            copies.append(copy)
+        return copies
+
+    def dots_end(copies, g):
+        for copy in copies:
+            copy.wait()
+        block = drecv[g, 0]
+        for k in range(1, lat_n):
+            block = block + drecv[g, k]
+        sums = jnp.sum(block, axis=1, keepdims=True)
+        return sums[0:1], sums[1:2]
+
+    lat_b.wait()
+    lat_a.wait()
+    for p in range(half):
+        lat_a2[p].wait()
+        rim_member(0, p)
+
+        def go(l, _):
+            lat_member(0, p, 0, l)
+            return 0
+
+        lax.fori_loop(0, levels, go, 0)
+
+    def go_cov(l, _):
+        cov_level(l)
+        return 0
+
+    lax.fori_loop(0, levels, go_cov, 0)
+    lat_s.wait()
+    lat_s2.wait()
+    cov_static(0)
+    sharing = share(0)
+    x_second.start()
+
+    out_level(0, 0, half)
+    stat_b = out_static(0)
+    cz = shared(sharing, 0)
+    z = [ow[s] * ov[s] for s in range(lon_n)]
+    q = [z[s] + ow[s] * cz[s] for s in range(lon_n)]
+    for s in range(lon_n):
+        scatter(s, q[s], 1)
+    lat_q = send_grid(1)
+    dots0 = dots_start(0, [z[s] * cz[s] for s in range(lon_n)], [cz[s] * q[s] for s in range(lon_n)])
+    x_second.wait()
+
+    def pack_second(p, _):
+        pack_member(p, all_rows, full)
+        return 0
+
+    lax.fori_loop(half, members, pack_second, 0)
+    lat_a3 = lat_members(second, all_rows)
+    lat_a3.start()
+    lat_q.wait()
+    rim_span(1, 0, half)
+
+    def go_q(l, _):
+        for p in range(half):
+            lat_member(1, p, 0, l)
+        cov_level(l)
+        return 0
+
+    lax.fori_loop(0, levels, go_q, 0)
+    cov_static(1)
+    sharing = share(1)
+    stat_q = out_static(1)
+    out_level(1, 0, half)
+    lat_a3.wait()
+    rim_span(0, half, half)
+    out_level(0, half, half)
+    b_out = pltpu.make_async_copy(ubuf.at[0], ub_ref, done.at[0])
+    b_out.start()
+    rim_span(1, half, half)
+    out_level(1, half, half)
+    q_out = pltpu.make_async_copy(ubuf.at[1], uq_ref, done.at[1])
+    q_out.start()
+
+    cq = shared(sharing, 1)
+    norm0, curve0 = dots_end(dots0, 0)
+    alpha0 = norm0 / curve0
+    resid = [z[s] - alpha0 * q[s] for s in range(lon_n)]
+    cr = [cz[s] - alpha0 * cq[s] for s in range(lon_n)]
+    dots1 = dots_start(
+        1,
+        [resid[s] * cr[s] for s in range(lon_n)],
+        [cr[s] * (resid[s] + ow[s] * cr[s]) for s in range(lon_n)],
+    )
+    for copy in [*stat_b, *stat_q]:
+        copy.wait()
+    s_out = pltpu.make_async_copy(stat, st_ref, done.at[2])
+    s_out.start()
+    norm1, curve1 = dots_end(dots1, 1)
+    beta = norm1 / norm0
+    alpha1 = norm1 / (curve1 - beta * norm1 / alpha0)
+    on_b = alpha0 + alpha1 * (1.0 + beta)
+    on_q = -alpha0 * alpha1
+    coef_ref[...] = jnp.where(iota((2, 128), 0) == 0, on_b, on_q)
+    for copy in (b_out, q_out, s_out):
+        copy.wait()
+
+
+def paired_device(anomalies, spread, obs_index, innovation, obs_weight, band_width):
+    members = anomalies.shape[0]
+    levels, lon_cells, lat_cells = spread.shape
+    sizes = tuple(lax.axis_size(a) for a in AXES)
+    lon_n, lat_n, mem_n = sizes
+    half = members // lon_n
+    full = lon_n * lon_cells
+    group = lon_n * mem_n
+    n_obs = obs_index.shape[-1]
+    v = pltpu.VMEM
+    sem = pltpu.SemaphoreType.DMA
+    wide = lat_cells
+    copies = 9 + 2 * (2 + 2 + half + 2 + 1) + 2 * (group - 1 + lat_n - 1 + mem_n - 1)
+    scratch = [
+        v((members, levels, full, wide), BF16),
+        v((members, full, 2 * wide), BF16),
+        v((members, full, wide), BF16),
+        v((members, full, wide), BF16),
+        v((full, wide), F32),
+        v((full, 2 * wide), F32),
+        v((2, full, wide), F32),
+        v((lon_n, 1, n_obs), jnp.int32),
+        v((lon_n, 1, n_obs), F32),
+        v((lon_n, 1, n_obs), F32),
+        v((lon_n, levels * lon_cells, n_obs), BF16),
+        v((2, levels, full, wide), F32),
+        v((2, full, 2 * wide), F32),
+        v((2, 2, full, wide), F32),
+        v((lon_n, levels * lon_cells, wide), F32),
+        v((2, group, lon_n, 1, n_obs), F32),
+        v((2, lat_n, 2, 128), F32),
+        v((2, levels, 2 * wide, 2 * wide), BF16),
+        v((2, levels, 4 * wide, 2 * wide), BF16),
+        v((levels, 2 * full, 2 * full), BF16),
+        v((levels, 2 * lon_cells, 2 * full), BF16),
+        v((members, full, 4 * wide), BF16),
+        v((levels, 2 * full, members * wide), BF16),
+        v((2, members, levels, lon_cells, wide), F32),
+        v((mem_n, 2, lon_cells, wide), F32),
+        sem((copies,)), sem((copies,)), sem((3,)),
+    ]
+    hbm = pl.BlockSpec(memory_space=pl.ANY)
+    kernel = functools.partial(paired, dims=(members, levels, lon_cells, lat_cells, sizes))
+    out = jax.ShapeDtypeStruct((members, levels, lon_cells, lat_cells), F32)
+    ub, uq, st, coef = pl.pallas_call(
+        kernel,
+        out_shape=[
+            out, out,
+            jax.ShapeDtypeStruct((levels, 2, lon_cells, lat_cells), F32),
+            jax.ShapeDtypeStruct((2, 128), F32),
+        ],
+        in_specs=[VMEM] * 5 + [pl.BlockSpec(memory_space=pltpu.SMEM)],
+        out_specs=[hbm, hbm, hbm, VMEM],
+        scratch_shapes=scratch,
+        compiler_params=pltpu.CompilerParams(
+            collective_id=0, has_side_effects=True, vmem_limit_bytes=48 * 2**20
+        ),
+    )(
+        anomalies, spread, obs_index.reshape(1, -1), obs_weight.reshape(1, -1),
+        innovation.reshape(1, -1), band_width,
+    )
+    on_b, on_q = coef[0, 0], coef[1, 0]
+    return on_b * ub + on_q * uq, on_b * st[:, 0] + on_q * st[:, 1]
+
+
+def pick(*args):
+    members = args[0].shape[0]
+    levels, lon_cells, lat_cells = args[1].shape
+    lon_n, lat_n, mem_n = (lax.axis_size(a) for a in AXES)
+    pairs = lon_n == 2 and members % 2 == 0 and levels == mem_n and lon_cells > BAND and lat_n > 1
+    return (paired_device if pairs else per_device)(*args)
+
+
 def solution(mesh):
     return jax.shard_map(
-        per_device,
+        pick,
         mesh=mesh,
         in_specs=(
             P("mem", None, "lon", "lat"),

time: 66.1 us -> 56.1 us (0.85)
  Pallas kernels: 62.2 us -> 45.4 us
  other arithmetic: 0 us -> 4.34 us
  local copies, waits for them, and re-layouts: 3 us -> 5.29 us
    pallas_call x1, Pallas kernels: 62.2 us -> 45.4 us  [paired_device(): pl.pallas_call(kernel, out_shape=[out, out, jax.ShapeDtypeStruct((levels,...]
    add x0 -> x2, other arithmetic: none -> 4.34 us  [paired_device(): return (on_b * ub + on_q * uq, on_b * st[:, 0] + on_q * st[:, 1])]
    unnamed x4 -> x12, local copies, waits for them, and re-layouts: 3 us -> 4.71 us
where the time goes in v1:
time: 56.1 us; the launch traced here: 55.7 us
  Pallas kernels  45.4 us (81%)
  local copies, waits for them, and re-layouts  5.29 us (9%)
  other arithmetic  4.34 us (8%)
  between operations  0.65 us (1%)
    pallas_call x1, Pallas kernels, paired_device(): pl.pallas_call(kernel, out_shape=[out, out, jax.ShapeDtypeStruct((levels,...  45.4 us
    unnamed x12, local copies, waits for them, and re-layouts  4.71 us
    add x2, other arithmetic, paired_device(): return (on_b * ub + on_q * uq, on_b * st[:, 0] + on_q * st[:, 1])  4.34 us

profile of v1, /device:TPU:0, one launch (start us, length us, event | category | flops | bytes accessed | tf_op | source)
XLA Modules:
  0.0 55.7 jit_solution(18235711344265072418)
XLA Ops:
  0.6 0.0 copy-start.5
  0.6 0.7 %copy-done.5 = s32[2,4]{1,0:T(2,128)S(1)} copy-done((s32[2,4]{1,0:T(2,128)S(1)}, s32[2,4]{1,0:T(2,128)}, u32[]{:S(2)}) %copy-start.5) | copy-done | bytes 56
  1.3 0.0 copy-start
  1.3 1.0 %copy-done = bf16[8,4,64,128]{3,2,1,0:T(8,128)(2,1)S(1)} copy-done((bf16[8,4,64,128]{3,2,1,0:T(8,128)(2,1)S(1)}, bf16[8,4,64,128]{3,2,1,0:T(8,128)(2,1)}, u32[]{:S(2)}) %copy-start) | copy-done | bytes 524312
  2.4 0.0 copy-start.1
  2.4 0.9 %copy-done.1 = f32[4,64,128]{2,1,0:T(8,128)S(1)} copy-done((f32[4,64,128]{2,1,0:T(8,128)S(1)}, f32[4,64,128]{2,1,0:T(8,128)}, u32[]{:S(2)}) %copy-start.1) | copy-done | bytes 131096
  3.3 0.0 copy-start.2
  3.3 0.7 %copy-done.2 = s32[1,1,2048]{2,1,0:T(1,128)S(1)} copy-done((s32[1,1,2048]{2,1,0:T(1,128)S(1)}, s32[1,1,2048]{2,1,0:T(1,128)}, u32[]{:S(2)}) %copy-start.2) | copy-done | bytes 8216
  4.0 0.0 copy-start.3
  4.0 0.7 %copy-done.3 = f32[1,1,2048]{2,1,0:T(1,128)S(1)} copy-done((f32[1,1,2048]{2,1,0:T(1,128)S(1)}, f32[1,1,2048]{2,1,0:T(1,128)}, u32[]{:S(2)}) %copy-start.3) | copy-done | bytes 8216
  4.7 0.0 copy-start.4
  4.7 0.7 %copy-done.4 = f32[1,1,2048]{2,1,0:T(1,128)S(1)} copy-done((f32[1,1,2048]{2,1,0:T(1,128)S(1)}, f32[1,1,2048]{2,1,0:T(1,128)}, u32[]{:S(2)}) %copy-start.4) | copy-done | bytes 8216
  5.4 45.4 %shard_map.77 = (f32[8,4,64,128]{3,2,1,0:T(8,128)S(1)}, f32[8,4,64,128]{3,2,1,0:T(8,128)S(1)}, f32[4,2,64,128]{3,2,1,0:T(8,128)S(1)}, f32[2,128]{1,0:T(2,128)S(1)}) custom-call(bf16[8,4,64,128]{3,2,1,0:T(8,128)(2,1)S(1)} %copy-done, f32[4,64,128]{2,1,0:T(8,128)S(1)} %copy-done.1, s32[1,2048]{1,0:T(1,128)S(1)} %bitcast.7, f32[1,2048]{1,0:T(1,128)S(1)} %bitcast.8, ...), custom_call_target="tpu_custom_call" | custom-call | tf_op jit(solution)/shard_map/pallas_call | solution.py:1073
  50.8 0.6 %fusion = (f32[1,1]{1,0:T(1,128)}, f32[1,1]{1,0:T(1,128)}) fusion(f32[2,128]{1,0:T(2,128)S(1)} %get-tuple-element.6), kind=kLoop, calls=%fused_computation.2 | loop fusion | bytes 16 | tf_op jit(solution)/shard_map/slice | solution.py:1090
  51.4 2.4 %multiply_add_fusion = f32[8,4,64,128]{3,2,1,0:T(8,128)} fusion(f32[8,4,64,128]{3,2,1,0:T(8,128)S(1)} %get-tuple-element.8, f32[8,4,64,128]{3,2,1,0:T(8,128)S(1)} %get-tuple-element.7, f32[]{:T(128)} %bitcast.4, f32[]{:T(128)} %bitcast.3), kind=kLoop, calls=%fused_computation | loop fusion | flops 786432 | bytes 3145736 | tf_op jit(solution)/shard_map/add | solution.py:1091
  53.8 1.9 %add_bitcast_fusion = f32[4,64,128]{2,1,0:T(8,128)} fusion(f32[4,2,64,128]{3,2,1,0:T(8,128)S(1)} %get-tuple-element.9, f32[]{:T(128)} %bitcast.4, f32[]{:T(128)} %bitcast.3), kind=kLoop, calls=%fused_computation.1 | loop fusion | flops 98304 | bytes 393224 | tf_op jit(solution)/shard_map/add | solution.py:1091
Async XLA Ops:
  0.6 0.7 %copy-start.5 = (s32[2,4]{1,0:T(2,128)S(1)}, s32[2,4]{1,0:T(2,128)}, u32[]{:S(2)}) copy-start(s32[2,4]{1,0:T(2,128)} %bw_ref.1) | copy-start | bytes 100
  1.3 1.0 %copy-start = (bf16[8,4,64,128]{3,2,1,0:T(8,128)(2,1)S(1)}, bf16[8,4,64,128]{3,2,1,0:T(8,128)(2,1)}, u32[]{:S(2)}) copy-start(bf16[8,4,64,128]{3,2,1,0:T(8,128)(2,1)} %a_ref.1) | copy-start | bytes 1572868
  2.4 0.9 %copy-start.1 = (f32[4,64,128]{2,1,0:T(8,128)S(1)}, f32[4,64,128]{2,1,0:T(8,128)}, u32[]{:S(2)}) copy-start(f32[4,64,128]{2,1,0:T(8,128)} %s_ref.1) | copy-start | bytes 393220
  3.3 0.7 %copy-start.2 = (s32[1,1,2048]{2,1,0:T(1,128)S(1)}, s32[1,1,2048]{2,1,0:T(1,128)}, u32[]{:S(2)}) copy-start(s32[1,1,2048]{2,1,0:T(1,128)} %param.8) | copy-start | bytes 24580
  4.0 0.7 %copy-start.3 = (f32[1,1,2048]{2,1,0:T(1,128)S(1)}, f32[1,1,2048]{2,1,0:T(1,128)}, u32[]{:S(2)}) copy-start(f32[1,1,2048]{2,1,0:T(1,128)} %param.10) | copy-start | bytes 24580
  4.7 0.7 %copy-start.4 = (f32[1,1,2048]{2,1,0:T(1,128)S(1)}, f32[1,1,2048]{2,1,0:T(1,128)}, u32[]{:S(2)}) copy-start(f32[1,1,2048]{2,1,0:T(1,128)} %param.9) | copy-start | bytes 24580

commit v2 on v1

--- a/solution.py
+++ b/solution.py
@@ -541,17 +541,19 @@
     )
 
 
-def paired(a_ref, s_ref, i_ref, w_ref, v_ref, bw_ref, ub_ref, uq_ref, st_ref, coef_ref, *scratch, dims):
+def paired(a_hbm, s_hbm, i_hbm, w_hbm, v_hbm, bw_hbm, ub_ref, uq_ref, st_ref, coef_ref, *scratch, dims):
     members, levels, lon_cells, lat_cells, sizes = dims
     (acen, arim, plo, phi, scen, srim, spack, oidx, ow, ov, at_row, grid, grim, gpack, cov, orecv,
-     drecv, mat_c, mat_r, lon_t, lon_l, xr, ts, ubuf, stat, send, recv, done) = scratch
+     drecv, mat_c, mat_r, lon_t, lon_l, xr, tc, ts, to, bw_ref, send, recv, load, relay) = scratch
     lon_n, lat_n, mem_n = sizes
     half = members // lon_n
     full = lon_n * lon_cells
     group = lon_n * mem_n
     rows = levels * lon_cells
     wide = lat_cells
-    n_obs = i_ref.shape[1]
+    edge = 16 * pl.cdiv(BAND, 16)
+    reach = lon_cells + 2 * edge
+    n_obs = oidx.shape[2]
     coef_ens = math.sqrt(hybrid_ens / (members * mem_n))
     coef_static = math.sqrt(hybrid_static)
     at_lon, lat_at, me = (lax.axis_index(a) for a in AXES)
@@ -566,11 +568,47 @@
     def lat_peer(step):
         return {"lat": lax.rem(lat_at + step, lat_n)}
 
+    own_rows, far_rows = pl.ds(0, lon_cells), pl.ds(lon_cells, lon_cells)
+    first, second = pl.ds(0, half), pl.ds(half, half)
+    loads = [
+        pltpu.make_async_copy(src, dst, load.at[k])
+        for k, (src, dst) in enumerate((
+            (i_hbm, oidx.at[0]),
+            (w_hbm, ow.at[0]),
+            (v_hbm, ov.at[0]),
+            (s_hbm.at[me], scen.at[own_rows]),
+            (a_hbm.at[pl.ds(other * half, half)], acen.at[second, :, own_rows, :]),
+            (a_hbm.at[pl.ds(at_lon * half, half)], acen.at[first, :, own_rows, :]),
+            (bw_hbm, bw_ref),
+        ))
+    ]
+    for copy in loads:
+        copy.start()
+
+    near = [
+        (True, {"lon": other}),
+        (has_low, {"lat": lat_at - 1}),
+        (has_high, {"lat": lat_at + 1}),
+        (me > 0, {"mem": me - 1}),
+        (me < mem_n - 1, {"mem": me + 1}),
+    ]
+    n_near = sum(jnp.asarray(there, jnp.int32) for there, _ in near)
+
+    def greet(sem):
+        for there, where in near:
+            def go(where=where):
+                pl.semaphore_signal(sem, inc=1, device_id=where, device_id_type=MESH)
+
+            go() if there is True else pl.when(there)(go)
+
+    def relay_round(r):
+        pl.semaphore_wait(relay.at[r], n_near)
+        if r + 1 < rounds:
+            greet(relay.at[r + 1])
+
+    rounds = max(lon_n + mem_n - 2, lat_n - 1) - 1
     barrier = pltpu.get_barrier_semaphore()
-    for step in range(1, group):
-        pl.semaphore_signal(barrier, inc=1, device_id=group_peer(step), device_id_type=MESH)
-    for step in range(1, lat_n):
-        pl.semaphore_signal(barrier, inc=1, device_id=lat_peer(step), device_id_type=MESH)
+    greet(barrier)
 
     used = [0]
 
@@ -585,8 +623,6 @@
     partner = {"lon": other}
     lat_low = {"lat": lax.rem(lat_at + lat_n - 1, lat_n)}
     lat_high = {"lat": lax.rem(lat_at + 1, lat_n)}
-    own_rows = pl.ds(pl.multiple_of(at_lon * lon_cells, lon_cells), lon_cells)
-    far_rows = pl.ds(pl.multiple_of(other * lon_cells, lon_cells), lon_cells)
     all_rows = pl.ds(0, full)
     low_lanes = pl.ds(0, wide)
     high_lanes = pl.ds(wide, wide)
@@ -623,10 +659,6 @@
     def actual(p):
         return lax.rem(at_lon * half + p, members)
 
-    def fill(p, _):
-        acen[p, :, own_rows, :] = a_ref[actual(p)]
-        return 0
-
     def pack_member(p, span, count):
         low, high = lane_pack(lambda l: acen[p, l, span, :].astype(F32), count)
         plo[p, span, :] = low.astype(BF16)
@@ -652,22 +684,19 @@
     def lat_grid(g):
         return Lat(gpack.at[g, 0], gpack.at[g, 1], grim.at[g, :, low_lanes], grim.at[g, :, high_lanes])
 
-    first, second = pl.ds(0, half), pl.ds(half, half)
-    x_obs = [
-        remote(src, dst.at[1], partner) for src, dst in ((i_ref, oidx), (w_ref, ow), (v_ref, ov))
+    x_obs = [remote(ref.at[0], ref.at[1], partner) for ref in (oidx, ow, ov)]
+    x_static = remote(scen.at[own_rows], scen.at[far_rows], partner)
+    x_first = [
+        remote(acen.at[half + p, :, own_rows, :], acen.at[p, :, far_rows, :], partner)
+        for p in range(half)
     ]
-    x_static = remote(s_ref.at[me], scen.at[own_rows], partner)
-    x_first = [
-        remote(a_ref.at[other * half + p], acen.at[p, :, own_rows, :], partner) for p in range(half)
-    ]
-    x_second = remote(
-        a_ref.at[pl.ds(at_lon * half, half)], acen.at[second, :, own_rows, :], partner
-    )
-    pl.semaphore_wait(barrier, group - 1 + lat_n - 1)
-    for copy in [*x_obs, x_static, *x_first]:
+    x_second = remote(acen.at[first, :, own_rows, :], acen.at[second, :, far_rows, :], partner)
+    for copy in loads:
+        copy.wait()
+    pl.semaphore_wait(barrier, n_near)
+    for copy in [*x_obs, *x_first, x_static]:
         copy.start()
-
-    lax.fori_loop(0, members, fill, 0)
+    greet(relay.at[0])
 
     def pack_first(p, _):
         pack_member(p, own_rows, lon_cells)
@@ -676,7 +705,6 @@
     lax.fori_loop(0, half, pack_first, 0)
     lat_a = lat_members(first, own_rows)
     lat_a.start()
-    scen[own_rows, :] = s_ref[me]
     pack_static(own_rows, lon_cells)
     lat_s = lat_static(own_rows)
     lat_s.start()
@@ -693,6 +721,7 @@
         srim[:, high_lanes] = jnp.zeros((full, wide), F32)
         grim[:, :, high_lanes] = jnp.zeros((2, full, wide), F32)
 
+    relay_round(0)
     slot_rows = (own_rows, far_rows)
     slot_tile = (at_lon, other)
 
@@ -715,7 +744,7 @@
             grid[g, l, slot_rows[s], :] = out[l * lon_cells : (l + 1) * lon_cells]
 
     def gather(s, g):
-        hi, lo = split2(cov[slot_tile[s]].T)
+        hi, lo = split2(cov[s].T)
         left = jnp.concatenate([hi, lo], axis=0)
         step = 512 if n_obs % 512 == 0 else n_obs
         for c in range(0, n_obs, step):
@@ -733,7 +762,6 @@
         copy.start()
         return copy
 
-    oidx[0], ow[0], ov[0] = i_ref[...], w_ref[...], v_ref[...]
     mark_rows(0)
     scatter(0, ow[0] * ov[0], 0)
 
@@ -751,21 +779,23 @@
 
         def put_lon(ref, count, value):
             hi, lo = split2(value)
-            ref[l, :count, :full] = hi
-            ref[l, :count, full:] = hi
-            ref[l, count:, :full] = lo
-            ref[l, count:, full:] = jnp.zeros((count, full), BF16)
+            cols = value.shape[1]
+            ref[l, :count, :] = jnp.concatenate([hi, hi], axis=1)
+            ref[l, count:, :] = jnp.concatenate([lo, jnp.zeros((count, cols), BF16)], axis=1)
 
         w = weights(0)
 
-        def ring(count, base):
-            d = iota((count, full), 1) - (iota((count, full), 0) + base)
+        def ring(count, cols):
+            c = iota((count, cols), 1)
+            if cols < full:
+                c = jnp.where(c < lon_cells + edge, c, c + full - cols)
+            d = c - iota((count, cols), 0)
             d = jnp.where(d > full // 2, d - full, d)
             return w(jnp.where(d < -(full // 2), d + full, d))
 
-        circle = split2(ring(full, 0))
+        circle = split2(ring(full, full))
         put_lon(lon_t, full, dot3(circle, circle))
-        put_lon(lon_l, lon_cells, ring(lon_cells, at_lon * lon_cells))
+        put_lon(lon_l, lon_cells, ring(lon_cells, reach))
 
         def put_lat(ref, kind, hi_at, lo_at, value):
             hi, lo = split2(value)
@@ -799,6 +829,8 @@
         return 0
 
     lax.fori_loop(0, levels, make_matrices, 0)
+    for r in range(1, rounds):
+        relay_round(r)
 
     for copy in x_obs:
         copy.wait()
@@ -806,10 +838,51 @@
     scatter(1, ow[1] * ov[1], 0)
     lat_b = send_grid(0)
 
-    x_static.wait()
-    pack_static(far_rows, lon_cells)
-    lat_s2 = lat_static(far_rows)
-    lat_s2.start()
+    def dot(a, b):
+        return jnp.dot(a, b, preferred_element_type=F32)
+
+    def fold(t):
+        return t[:, :wide] + t[:, wide:]
+
+    def pair(x):
+        return jnp.concatenate(split2(x), axis=1)
+
+    def stack(x):
+        return jnp.concatenate(split2(x), axis=0)
+
+    def reached(x):
+        return jnp.concatenate([x[: lon_cells + edge], x[full - edge :]], axis=0)
+
+    def rim_member(g, p):
+        xr[p] = pair(arim[p].astype(F32) * grim[g])
+
+    def center_member(g, p):
+        for l in range(levels):
+            tc[p, l] = fold(dot(pair(acen[p, l].astype(F32) * grid[g, l]), mat_c[0, l]))
+
+    def lat_member(p, at):
+        for l in range(levels):
+            ts[l, :, at] = stack(tc[p, l] + fold(dot(xr[p], mat_r[0, l])))
+
+    def cov_level(l):
+        u = dot(lon_t[l], ts[l])
+        u = u[:full] + u[full:]
+        acc = acen[0, l].astype(F32) * u[:, :wide]
+        for p in range(1, half):
+            acc = acc + acen[p, l].astype(F32) * u[:, p * wide : (p + 1) * wide]
+        acc = acc * (coef_ens * coef_ens)
+        for j in range(lon_n):
+            cov[j, l * lon_cells : (l + 1) * lon_cells, :] = acc[j * lon_cells : (j + 1) * lon_cells]
+
+    def cov_static(g):
+        t = dot(pair(scen[...] * grid[g, me]), mat_c[0, me])
+        t = t + dot(pair(srim[...] * grim[g]), mat_r[0, me])
+        u = dot(lon_t[me], stack(fold(t)))
+        acc = scen[...] * (u[:full] + u[full:]) * (coef_static**2 / lon_n)
+        at = pl.ds(pl.multiple_of(me * lon_cells, lon_cells), lon_cells)
+        for j in range(lon_n):
+            cov[j, at, :] = cov[j, at, :] + acc[j * lon_cells : (j + 1) * lon_cells]
+
     lat_a2 = []
     for p in range(half):
         x_first[p].wait()
@@ -817,48 +890,12 @@
         copy = lat_members(p, far_rows)
         copy.start()
         lat_a2.append(copy)
-
-    def dot(a, b):
-        return jnp.dot(a, b, preferred_element_type=F32)
-
-    def rim_split(x):
-        hi, lo = split2(x)
-        return jnp.concatenate([hi, lo], axis=1)
-
-    def rim_member(g, p):
-        xr[p] = rim_split(arim[p].astype(F32) * grim[g])
-
-    def along_lat(x, rims, kind, l):
-        t = dot(rim_split(x), mat_c[kind, l]) + dot(rims, mat_r[kind, l])
-        return split2(t[:, :wide] + t[:, wide:])
-
-    def lat_member(g, p, kind, l):
-        hi, lo = along_lat(acen[p, l].astype(F32) * grid[g, l], xr[p], kind, l)
-        ts[l, :full, p * wide : (p + 1) * wide] = hi
-        ts[l, full:, p * wide : (p + 1) * wide] = lo
-
-    def lat_own_static(g, kind):
-        rims = rim_split(srim[...] * grim[g])
-        hi, lo = along_lat(scen[...] * grid[g, me], rims, kind, me)
-        return jnp.concatenate([hi, lo], axis=0)
-
-    def cov_level(l):
-        u = dot(lon_t[l], ts[l, :, : half * wide])
-        u = u[:full] + u[full:]
-        acc = acen[0, l].astype(F32) * u[:, :wide]
-        for p in range(1, half):
-            acc = acc + acen[p, l].astype(F32) * u[:, p * wide : (p + 1) * wide]
-        acc = acc * (coef_ens * coef_ens)
-        at = pl.ds(pl.multiple_of(l * lon_cells, lon_cells), lon_cells)
-        for j in range(lon_n):
-            cov[j, at, :] = acc[j * lon_cells : (j + 1) * lon_cells]
-
-    def cov_static(g):
-        u = dot(lon_t[me], lat_own_static(g, 0))
-        acc = scen[...] * (u[:full] + u[full:]) * (coef_static**2 / lon_n)
-        at = pl.ds(pl.multiple_of(me * lon_cells, lon_cells), lon_cells)
-        for j in range(lon_n):
-            cov[j, at, :] = cov[j, at, :] + acc[j * lon_cells : (j + 1) * lon_cells]
+        center_member(0, p)
+    x_static.wait()
+    x_second.start()
+    pack_static(far_rows, lon_cells)
+    lat_s2 = lat_static(far_rows)
+    lat_s2.start()
 
     def share(g):
         for s in range(lon_n):
@@ -882,13 +919,17 @@
         return sums
 
     def out_level(g, p0, n):
+        out_ref = (ub_ref, uq_ref)[g]
+
         def go(l, _):
-            for p in range(p0, p0 + n):
-                lat_member(g, p, 1, l)
-            u = dot(lon_l[l], ts[l, :, p0 * wide : (p0 + n) * wide])
+            for p in range(n):
+                x = reached(acen[p0 + p, l]).astype(F32) * reached(grid[g, l])
+                t = dot(pair(x), mat_c[1, l]) + dot(reached(xr[p0 + p]), mat_r[1, l])
+                to[l, :, p * wide : (p + 1) * wide] = stack(fold(t))
+            u = dot(lon_l[l], to[l])
             u = (u[:lon_cells] + u[lon_cells:]) * coef_ens
             for p in range(n):
-                ubuf[g, actual(p0 + p), l] = u[:, p * wide : (p + 1) * wide]
+                out_ref[actual(p0 + p), l] = u[:, p * wide : (p + 1) * wide]
             return 0
 
         lax.fori_loop(0, levels, go, 0)
@@ -901,11 +942,13 @@
         lax.fori_loop(p0, p0 + n, go, 0)
 
     def out_static(g):
-        u = dot(lon_l[me], lat_own_static(g, 1))
-        stat[me, g] = (u[:lon_cells] + u[lon_cells:]) * coef_static
+        t = dot(pair(reached(scen[...] * grid[g, me])), mat_c[1, me])
+        t = t + dot(pair(reached(srim[...] * grim[g])), mat_r[1, me])
+        u = dot(lon_l[me], stack(fold(t)))
+        st_ref[g, me] = (u[:lon_cells] + u[lon_cells:]) * coef_static
         copies = []
         for j in range(1, mem_n):
-            copy = remote(stat.at[me, g], stat.at[me, g], {"mem": lax.rem(me + j, mem_n)})
+            copy = remote(st_ref.at[g, me], st_ref.at[g, me], {"mem": lax.rem(me + j, mem_n)})
             copy.start()
             copies.append(copy)
         return copies
@@ -937,31 +980,35 @@
         sums = jnp.sum(block, axis=1, keepdims=True)
         return sums[0:1], sums[1:2]
 
+    def lat_all(p, _):
+        lat_member(p, pl.ds(pl.multiple_of(p * wide, wide), wide))
+        return 0
+
     lat_b.wait()
     lat_a.wait()
     for p in range(half):
         lat_a2[p].wait()
         rim_member(0, p)
-
-        def go(l, _):
-            lat_member(0, p, 0, l)
-            return 0
-
-        lax.fori_loop(0, levels, go, 0)
-
-    def go_cov(l, _):
+        lat_member(p, slice(p * wide, (p + 1) * wide))
+    for l in range(levels):
         cov_level(l)
-        return 0
-
-    lax.fori_loop(0, levels, go_cov, 0)
     lat_s.wait()
     lat_s2.wait()
     cov_static(0)
     sharing = share(0)
-    x_second.start()
-
+
+    x_second.wait()
+
+    def pack_second(p, _):
+        pack_member(p, all_rows, full)
+        return 0
+
+    lax.fori_loop(half, members, pack_second, 0)
+    lat_a3 = lat_members(second, all_rows)
+    lat_a3.start()
     out_level(0, 0, half)
     stat_b = out_static(0)
+
     cz = shared(sharing, 0)
     z = [ow[s] * ov[s] for s in range(lon_n)]
     q = [z[s] + ow[s] * cz[s] for s in range(lon_n)]
@@ -969,38 +1016,27 @@
         scatter(s, q[s], 1)
     lat_q = send_grid(1)
     dots0 = dots_start(0, [z[s] * cz[s] for s in range(lon_n)], [cz[s] * q[s] for s in range(lon_n)])
-    x_second.wait()
-
-    def pack_second(p, _):
-        pack_member(p, all_rows, full)
+
+    def center_all(p, _):
+        center_member(1, p)
         return 0
 
-    lax.fori_loop(half, members, pack_second, 0)
-    lat_a3 = lat_members(second, all_rows)
-    lat_a3.start()
+    lax.fori_loop(0, half, center_all, 0)
+    lat_a3.wait()
+    rim_span(0, half, half)
+    out_level(0, half, half)
+
     lat_q.wait()
     rim_span(1, 0, half)
-
-    def go_q(l, _):
-        for p in range(half):
-            lat_member(1, p, 0, l)
+    lax.fori_loop(0, half, lat_all, 0)
+    for l in range(levels):
         cov_level(l)
-        return 0
-
-    lax.fori_loop(0, levels, go_q, 0)
     cov_static(1)
     sharing = share(1)
     stat_q = out_static(1)
     out_level(1, 0, half)
-    lat_a3.wait()
-    rim_span(0, half, half)
-    out_level(0, half, half)
-    b_out = pltpu.make_async_copy(ubuf.at[0], ub_ref, done.at[0])
-    b_out.start()
     rim_span(1, half, half)
     out_level(1, half, half)
-    q_out = pltpu.make_async_copy(ubuf.at[1], uq_ref, done.at[1])
-    q_out.start()
 
     cq = shared(sharing, 1)
     norm0, curve0 = dots_end(dots0, 0)
@@ -1014,15 +1050,26 @@
     )
     for copy in [*stat_b, *stat_q]:
         copy.wait()
-    s_out = pltpu.make_async_copy(stat, st_ref, done.at[2])
-    s_out.start()
     norm1, curve1 = dots_end(dots1, 1)
     beta = norm1 / norm0
     alpha1 = norm1 / (curve1 - beta * norm1 / alpha0)
     on_b = alpha0 + alpha1 * (1.0 + beta)
     on_q = -alpha0 * alpha1
     coef_ref[...] = jnp.where(iota((2, 128), 0) == 0, on_b, on_q)
-    for copy in (b_out, q_out, s_out):
+
+
+def combine(ub_ref, uq_ref, st_ref, coef_ref, ens_ref, static_ref, ens, static, sems):
+    on_b, on_q = coef_ref[0:1, :], coef_ref[1:2, :]
+    members = ens.shape[0]
+    copies = []
+    for m in range(members):
+        ens[m] = on_b * ub_ref[m] + on_q * uq_ref[m]
+        copies.append(pltpu.make_async_copy(ens.at[m], ens_ref.at[m], sems.at[m]))
+        copies[-1].start()
+    static[...] = on_b * st_ref[0] + on_q * st_ref[1]
+    copies.append(pltpu.make_async_copy(static, static_ref, sems.at[members]))
+    copies[-1].start()
+    for copy in copies:
         copy.wait()
 
 
@@ -1038,6 +1085,7 @@
     v = pltpu.VMEM
     sem = pltpu.SemaphoreType.DMA
     wide = lat_cells
+    reach = lon_cells + 2 * 16 * pl.cdiv(BAND, 16)
     copies = 9 + 2 * (2 + 2 + half + 2 + 1) + 2 * (group - 1 + lat_n - 1 + mem_n - 1)
     scratch = [
         v((members, levels, full, wide), BF16),
@@ -1060,42 +1108,56 @@
         v((2, levels, 2 * wide, 2 * wide), BF16),
         v((2, levels, 4 * wide, 2 * wide), BF16),
         v((levels, 2 * full, 2 * full), BF16),
-        v((levels, 2 * lon_cells, 2 * full), BF16),
+        v((levels, 2 * lon_cells, 2 * reach), BF16),
         v((members, full, 4 * wide), BF16),
-        v((levels, 2 * full, members * wide), BF16),
-        v((2, members, levels, lon_cells, wide), F32),
-        v((mem_n, 2, lon_cells, wide), F32),
-        sem((copies,)), sem((copies,)), sem((3,)),
+        v((half, levels, full, wide), F32),
+        v((levels, 2 * full, half * wide), BF16),
+        v((levels, 2 * reach, half * wide), BF16),
+        pltpu.SMEM(band_width.shape, jnp.int32),
+        sem((copies,)), sem((copies,)), sem((7,)),
+        pltpu.SemaphoreType.REGULAR((max(lon_n + mem_n - 2, lat_n - 1) - 1,)),
     ]
-    hbm = pl.BlockSpec(memory_space=pl.ANY)
+    hbm = pl.BlockSpec(memory_space=pltpu.HBM)
     kernel = functools.partial(paired, dims=(members, levels, lon_cells, lat_cells, sizes))
-    out = jax.ShapeDtypeStruct((members, levels, lon_cells, lat_cells), F32)
-    ub, uq, st, coef = pl.pallas_call(
+    ens = jax.ShapeDtypeStruct((members, levels, lon_cells, lat_cells), F32)
+    static = jax.ShapeDtypeStruct((levels, lon_cells, lat_cells), F32)
+    parts = pl.pallas_call(
         kernel,
         out_shape=[
-            out, out,
-            jax.ShapeDtypeStruct((levels, 2, lon_cells, lat_cells), F32),
+            ens, ens,
+            jax.ShapeDtypeStruct((2, levels, lon_cells, lat_cells), F32),
             jax.ShapeDtypeStruct((2, 128), F32),
         ],
-        in_specs=[VMEM] * 5 + [pl.BlockSpec(memory_space=pltpu.SMEM)],
-        out_specs=[hbm, hbm, hbm, VMEM],
+        in_specs=[hbm] * 6,
+        out_specs=[VMEM] * 4,
         scratch_shapes=scratch,
         compiler_params=pltpu.CompilerParams(
             collective_id=0, has_side_effects=True, vmem_limit_bytes=48 * 2**20
         ),
-    )(
-        anomalies, spread, obs_index.reshape(1, -1), obs_weight.reshape(1, -1),
-        innovation.reshape(1, -1), band_width,
-    )
-    on_b, on_q = coef[0, 0], coef[1, 0]
-    return on_b * ub + on_q * uq, on_b * st[:, 0] + on_q * st[:, 1]
+    )(*(
+        pltpu.with_memory_space_constraint(x, pltpu.HBM)
+        for x in (
+            anomalies, spread, obs_index.reshape(1, -1), obs_weight.reshape(1, -1),
+            innovation.reshape(1, -1), band_width,
+        )
+    ))
+    return pl.pallas_call(
+        combine,
+        out_shape=[ens, static],
+        in_specs=[VMEM] * 4,
+        out_specs=[hbm] * 2,
+        scratch_shapes=[
+            v(ens.shape, F32), v(static.shape, F32), sem((members + 1,)),
+        ],
+        compiler_params=pltpu.CompilerParams(vmem_limit_bytes=8 * 2**20),
+    )(*parts)
 
 
 def pick(*args):
     members = args[0].shape[0]
     levels, lon_cells, lat_cells = args[1].shape
     lon_n, lat_n, mem_n = (lax.axis_size(a) for a in AXES)
-    pairs = lon_n == 2 and members % 2 == 0 and levels == mem_n and lon_cells > BAND and lat_n > 1
+    pairs = lon_n == 2 and members % 2 == 0 and levels == mem_n and lon_cells % 32 == 0 and lat_n > 2
     return (paired_device if pairs else per_device)(*args)
 
 

time: 56.1 us -> 43.2 us (0.77)
  local copies, waits for them, and re-layouts: 5.29 us -> 0 us
  other arithmetic: 4.34 us -> 0 us
  Pallas kernels: 45.4 us -> 42.4 us
    unnamed x12 -> x0, local copies, waits for them, and re-layouts: 4.71 us -> none
    add x2 -> x0, other arithmetic: 4.34 us -> none  [paired_device(): return (on_b * ub + on_q * uq, on_b * st[:, 0] + on_q * st[:, 1])]
    pallas_call x1 -> x2, Pallas kernels: 45.4 us -> 42.4 us  [the longest x1 41.3 us: paired_device(): pl.pallas_call(kernel, out_shape=[ens, ens, jax.ShapeDtypeStruct((2, leve...]
    slice x1 -> x0, local copies, waits for them, and re-layouts: 0.59 us -> none  [paired_device(): on_b, on_q = (coef[0, 0], coef[1, 0])]
where the time goes in v2:
time: 43.2 us; the launch traced here: 43 us
  Pallas kernels  42.4 us (98%)
  between operations  0.64 us (1%)
    pallas_call x1, Pallas kernels, paired_device(): pl.pallas_call(kernel, out_shape=[ens, ens, jax.ShapeDtypeStruct((2, leve...  41.3 us
    pallas_call x1, Pallas kernels, paired_device(): pl.pallas_call(combine, out_shape=[ens, static], in_specs=[VMEM] * 4, out...  1.1 us

profile of v2, /device:TPU:0, one launch (start us, length us, event | category | flops | bytes accessed | tf_op | source)
XLA Modules:
  0.0 43.0 jit_solution(2627794782600499426)
XLA Ops:
  0.6 41.3 %shard_map.77 = (f32[8,4,64,128]{3,2,1,0:T(8,128)S(1)}, f32[8,4,64,128]{3,2,1,0:T(8,128)S(1)}, f32[2,4,64,128]{3,2,1,0:T(8,128)S(1)}, f32[2,128]{1,0:T(2,128)S(1)}) custom-call(bf16[8,4,64,128]{3,2,1,0:T(8,128)(2,1)} %a_hbm.1, f32[4,64,128]{2,1,0:T(8,128)} %s_hbm.1, s32[1,2048]{1,0:T(1,128)} %bitcast.3, f32[1,2048]{1,0:T(1,128)} %bitcast.4, ...), custom_call_target="tpu_custom_call" | custom-call | tf_op jit(solution)/shard_map/pallas_call | solution.py:1124
  41.9 1.1 %shard_map.78 = (f32[8,4,64,128]{3,2,1,0:T(8,128)}, f32[4,64,128]{2,1,0:T(8,128)}) custom-call(f32[8,4,64,128]{3,2,1,0:T(8,128)S(1)} %get-tuple-element.6.ub_ref, f32[8,4,64,128]{3,2,1,0:T(8,128)S(1)} %get-tuple-element.7.uq_ref, f32[2,4,64,128]{3,2,1,0:T(8,128)S(1)} %get-tuple-element.8.st_ref, f32[2,128]{1,0:T(2,128)S(1)} %get-tuple-element.9.coef_ref), custom_call_target="tpu_custom_call" | custom-call | tf_op jit(solution)/shard_map/pallas_call | solution.py:1144

commit v3 on v2

--- a/solution.py
+++ b/solution.py
@@ -543,8 +543,8 @@
 
 def paired(a_hbm, s_hbm, i_hbm, w_hbm, v_hbm, bw_hbm, ub_ref, uq_ref, st_ref, coef_ref, *scratch, dims):
     members, levels, lon_cells, lat_cells, sizes = dims
-    (acen, arim, plo, phi, scen, srim, spack, oidx, ow, ov, at_row, grid, grim, gpack, cov, orecv,
-     drecv, mat_c, mat_r, lon_t, lon_l, xr, tc, ts, to, bw_ref, send, recv, load, relay) = scratch
+    (acen, arim, plo, phi, sfull, sedge, srim, srims, spack, spacks, oidx, ow, ov, at_row, grid, grim, gpack, cov, orecv,
+     drecv, mat_c, mat_r, lon_t, lon_l, xr, xq, xo, tc, ts, to, bw_ref, send, recv, load, relay) = scratch
     lon_n, lat_n, mem_n = sizes
     half = members // lon_n
     full = lon_n * lon_cells
@@ -576,7 +576,7 @@
             (i_hbm, oidx.at[0]),
             (w_hbm, ow.at[0]),
             (v_hbm, ov.at[0]),
-            (s_hbm.at[me], scen.at[own_rows]),
+            (s_hbm, sfull.at[:, own_rows]),
             (a_hbm.at[pl.ds(other * half, half)], acen.at[second, :, own_rows, :]),
             (a_hbm.at[pl.ds(at_lon * half, half)], acen.at[first, :, own_rows, :]),
             (bw_hbm, bw_ref),
@@ -623,7 +623,6 @@
     partner = {"lon": other}
     lat_low = {"lat": lax.rem(lat_at + lat_n - 1, lat_n)}
     lat_high = {"lat": lax.rem(lat_at + 1, lat_n)}
-    all_rows = pl.ds(0, full)
     low_lanes = pl.ds(0, wide)
     high_lanes = pl.ds(wide, wide)
 
@@ -656,18 +655,20 @@
             high = jnp.where(here, pltpu.roll(x, lax.rem((l + 1) * RIM, wide), 1), high)
         return low, high
 
-    def actual(p):
-        return lax.rem(at_lon * half + p, members)
-
     def pack_member(p, span, count):
         low, high = lane_pack(lambda l: acen[p, l, span, :].astype(F32), count)
         plo[p, span, :] = low.astype(BF16)
         phi[p, span, :] = high.astype(BF16)
 
     def pack_static(span, count):
-        low, high = lane_pack(lambda l: scen[span, :], count, [me])
+        low, high = lane_pack(lambda l: sfull[me, span, :], count, [me])
         spack[0, span, :] = low
         spack[1, span, :] = high
+
+    def pack_statics(ref, span, to_span, count):
+        low, high = lane_pack(lambda l: ref[l, span, :], count)
+        spacks[0, to_span, :] = low
+        spacks[1, to_span, :] = high
 
     def lat_members(which, span):
         return Lat(
@@ -675,22 +676,27 @@
             arim.at[which, span, low_lanes], arim.at[which, span, high_lanes],
         )
 
-    def lat_static(span):
+    def lat_static(span, pack=spack, rim=srim):
         return Lat(
-            spack.at[0, span, :], spack.at[1, span, :],
-            srim.at[span, low_lanes], srim.at[span, high_lanes],
+            pack.at[0, span, :], pack.at[1, span, :],
+            rim.at[span, low_lanes], rim.at[span, high_lanes],
         )
 
     def lat_grid(g):
         return Lat(gpack.at[g, 0], gpack.at[g, 1], grim.at[g, :, low_lanes], grim.at[g, :, high_lanes])
 
     x_obs = [remote(ref.at[0], ref.at[1], partner) for ref in (oidx, ow, ov)]
-    x_static = remote(scen.at[own_rows], scen.at[far_rows], partner)
+    x_static = remote(sfull.at[me, own_rows], sfull.at[me, far_rows], partner)
     x_first = [
         remote(acen.at[half + p, :, own_rows, :], acen.at[p, :, far_rows, :], partner)
         for p in range(half)
     ]
-    x_second = remote(acen.at[first, :, own_rows, :], acen.at[second, :, far_rows, :], partner)
+    edges = pl.ds(lon_cells, 2 * edge)
+    x_edge = []
+    for src, k in ((0, 0), (lon_cells - edge, edge)):
+        src, dst = pl.ds(src, edge), pl.ds(lon_cells + k, edge)
+        x_edge.append(remote(acen.at[first, :, src, :], acen.at[second, :, dst, :], partner))
+        x_edge.append(remote(sfull.at[:, src], sedge.at[:, pl.ds(k, edge)], partner))
     for copy in loads:
         copy.wait()
     pl.semaphore_wait(barrier, n_near)
@@ -708,17 +714,25 @@
     pack_static(own_rows, lon_cells)
     lat_s = lat_static(own_rows)
     lat_s.start()
+    lax.fori_loop(half, members, pack_first, 0)
+    lat_a3 = lat_members(second, own_rows)
+    lat_a3.start()
+    pack_statics(sfull, own_rows, own_rows, lon_cells)
+    lat_s3 = lat_static(own_rows, spacks, srims)
+    lat_s3.start()
 
     @pl.when(jnp.logical_not(has_low))
     def _():
         arim[:, :, low_lanes] = jnp.zeros((members, full, wide), BF16)
         srim[:, low_lanes] = jnp.zeros((full, wide), F32)
+        srims[:, low_lanes] = jnp.zeros((reach, wide), F32)
         grim[:, :, low_lanes] = jnp.zeros((2, full, wide), F32)
 
     @pl.when(jnp.logical_not(has_high))
     def _():
         arim[:, :, high_lanes] = jnp.zeros((members, full, wide), BF16)
         srim[:, high_lanes] = jnp.zeros((full, wide), F32)
+        srims[:, high_lanes] = jnp.zeros((reach, wide), F32)
         grim[:, :, high_lanes] = jnp.zeros((2, full, wide), F32)
 
     relay_round(0)
@@ -875,10 +889,10 @@
             cov[j, l * lon_cells : (l + 1) * lon_cells, :] = acc[j * lon_cells : (j + 1) * lon_cells]
 
     def cov_static(g):
-        t = dot(pair(scen[...] * grid[g, me]), mat_c[0, me])
+        t = dot(pair(sfull[me] * grid[g, me]), mat_c[0, me])
         t = t + dot(pair(srim[...] * grim[g]), mat_r[0, me])
         u = dot(lon_t[me], stack(fold(t)))
-        acc = scen[...] * (u[:full] + u[full:]) * (coef_static**2 / lon_n)
+        acc = sfull[me] * (u[:full] + u[full:]) * (coef_static**2 / lon_n)
         at = pl.ds(pl.multiple_of(me * lon_cells, lon_cells), lon_cells)
         for j in range(lon_n):
             cov[j, at, :] = cov[j, at, :] + acc[j * lon_cells : (j + 1) * lon_cells]
@@ -892,7 +906,8 @@
         lat_a2.append(copy)
         center_member(0, p)
     x_static.wait()
-    x_second.start()
+    for copy in x_edge:
+        copy.start()
     pack_static(far_rows, lon_cells)
     lat_s2 = lat_static(far_rows)
     lat_s2.start()
@@ -918,40 +933,47 @@
             sums.append(acc)
         return sums
 
-    def out_level(g, p0, n):
+    def out_rows(l, cells, reads):
+        n = len(reads)
+        for p, read in enumerate(reads):
+            xo[p * reach : (p + 1) * reach] = pair(read() * cells)
+        t = fold(dot(xo[: n * reach], mat_c[1, l]) + dot(xq[: n * reach], mat_r[1, l]))
+        for p in range(n):
+            to[l, :, p * wide : (p + 1) * wide] = stack(t[p * reach : (p + 1) * reach])
+        u = dot(lon_l[l], to[l, :, : n * wide])
+        u = u[:lon_cells] + u[lon_cells:]
+        return [u[:, p * wide : (p + 1) * wide] for p in range(n)]
+
+    def out_first(g):
         out_ref = (ub_ref, uq_ref)[g]
+        for p in range(half):
+            xq[p * reach : (p + 1) * reach] = reached(xr[p])
 
         def go(l, _):
-            for p in range(n):
-                x = reached(acen[p0 + p, l]).astype(F32) * reached(grid[g, l])
-                t = dot(pair(x), mat_c[1, l]) + dot(reached(xr[p0 + p]), mat_r[1, l])
-                to[l, :, p * wide : (p + 1) * wide] = stack(fold(t))
-            u = dot(lon_l[l], to[l])
-            u = (u[:lon_cells] + u[lon_cells:]) * coef_ens
-            for p in range(n):
-                out_ref[actual(p0 + p), l] = u[:, p * wide : (p + 1) * wide]
+            reads = [lambda p=p: reached(acen[p, l]).astype(F32) for p in range(half)]
+            for p, u in enumerate(out_rows(l, reached(grid[g, l]), reads)):
+                out_ref[at_lon * half + p, l] = u * coef_ens
             return 0
 
         lax.fori_loop(0, levels, go, 0)
 
-    def rim_span(g, p0, n):
-        def go(p, _):
-            rim_member(g, p)
+    def out_second(g):
+        out_ref = (ub_ref, uq_ref)[g]
+        near_rim = reached(grim[g])
+        for p in range(half):
+            xq[p * reach : (p + 1) * reach] = pair(arim[half + p, :reach].astype(F32) * near_rim)
+        xq[half * reach :] = pair(srims[...] * near_rim)
+
+        def go(l, _):
+            reads = [lambda p=p: acen[half + p, l, :reach].astype(F32) for p in range(half)]
+            reads.append(lambda: jnp.concatenate([sfull[l, :lon_cells], sedge[l]], axis=0))
+            us = out_rows(l, reached(grid[g, l]), reads)
+            for p in range(half):
+                out_ref[other * half + p, l] = us[p] * coef_ens
+            st_ref[g, l] = us[half] * coef_static
             return 0
 
-        lax.fori_loop(p0, p0 + n, go, 0)
-
-    def out_static(g):
-        t = dot(pair(reached(scen[...] * grid[g, me])), mat_c[1, me])
-        t = t + dot(pair(reached(srim[...] * grim[g])), mat_r[1, me])
-        u = dot(lon_l[me], stack(fold(t)))
-        st_ref[g, me] = (u[:lon_cells] + u[lon_cells:]) * coef_static
-        copies = []
-        for j in range(1, mem_n):
-            copy = remote(st_ref.at[g, me], st_ref.at[g, me], {"mem": lax.rem(me + j, mem_n)})
-            copy.start()
-            copies.append(copy)
-        return copies
+        lax.fori_loop(0, levels, go, 0)
 
     def dots_start(g, left, right):
         def total(pairs):
@@ -980,34 +1002,46 @@
         sums = jnp.sum(block, axis=1, keepdims=True)
         return sums[0:1], sums[1:2]
 
-    def lat_all(p, _):
-        lat_member(p, pl.ds(pl.multiple_of(p * wide, wide), wide))
-        return 0
+    def rim_and_cov(g):
+        for p in range(half):
+            if g == 0:
+                lat_a2[p].wait()
+            rim_member(g, p)
+            if g == 0:
+                lat_member(p, slice(p * wide, (p + 1) * wide))
+        if g > 0:
+            rims = xr[:half].reshape(half * full, 4 * wide)
+            for l in range(levels):
+                t = fold(dot(rims, mat_r[0, l]))
+                for p in range(half):
+                    part = tc[p, l] + t[p * full : (p + 1) * full]
+                    ts[l, :, p * wide : (p + 1) * wide] = stack(part)
+        for l in range(levels):
+            cov_level(l)
+        if g == 0:
+            lat_s.wait()
+            lat_s2.wait()
+        cov_static(g)
+        return share(g)
 
     lat_b.wait()
     lat_a.wait()
-    for p in range(half):
-        lat_a2[p].wait()
-        rim_member(0, p)
-        lat_member(p, slice(p * wide, (p + 1) * wide))
-    for l in range(levels):
-        cov_level(l)
-    lat_s.wait()
-    lat_s2.wait()
-    cov_static(0)
-    sharing = share(0)
-
-    x_second.wait()
+    sharing = rim_and_cov(0)
+
+    for copy in x_edge:
+        copy.wait()
 
     def pack_second(p, _):
-        pack_member(p, all_rows, full)
+        pack_member(p, edges, 2 * edge)
         return 0
 
     lax.fori_loop(half, members, pack_second, 0)
-    lat_a3 = lat_members(second, all_rows)
-    lat_a3.start()
-    out_level(0, 0, half)
-    stat_b = out_static(0)
+    lat_a4 = lat_members(second, edges)
+    lat_a4.start()
+    pack_statics(sedge, slice(None), edges, 2 * edge)
+    lat_s4 = lat_static(edges, spacks, srims)
+    lat_s4.start()
+    out_first(0)
 
     cz = shared(sharing, 0)
     z = [ow[s] * ov[s] for s in range(lon_n)]
@@ -1017,26 +1051,23 @@
     lat_q = send_grid(1)
     dots0 = dots_start(0, [z[s] * cz[s] for s in range(lon_n)], [cz[s] * q[s] for s in range(lon_n)])
 
-    def center_all(p, _):
-        center_member(1, p)
+    def center_all(l, _):
+        for p in range(half):
+            xo[p * full : (p + 1) * full] = pair(acen[p, l].astype(F32) * grid[1, l])
+        t = fold(dot(xo[: half * full], mat_c[0, l]))
+        for p in range(half):
+            tc[p, l] = t[p * full : (p + 1) * full]
         return 0
 
-    lax.fori_loop(0, half, center_all, 0)
-    lat_a3.wait()
-    rim_span(0, half, half)
-    out_level(0, half, half)
+    lax.fori_loop(0, levels, center_all, 0)
+    for copy in (lat_a3, lat_a4, lat_s3, lat_s4):
+        copy.wait()
+    out_second(0)
 
     lat_q.wait()
-    rim_span(1, 0, half)
-    lax.fori_loop(0, half, lat_all, 0)
-    for l in range(levels):
-        cov_level(l)
-    cov_static(1)
-    sharing = share(1)
-    stat_q = out_static(1)
-    out_level(1, 0, half)
-    rim_span(1, half, half)
-    out_level(1, half, half)
+    sharing = rim_and_cov(1)
+    out_first(1)
+    out_second(1)
 
     cq = shared(sharing, 1)
     norm0, curve0 = dots_end(dots0, 0)
@@ -1048,8 +1079,6 @@
         [resid[s] * cr[s] for s in range(lon_n)],
         [cr[s] * (resid[s] + ow[s] * cr[s]) for s in range(lon_n)],
     )
-    for copy in [*stat_b, *stat_q]:
-        copy.wait()
     norm1, curve1 = dots_end(dots1, 1)
     beta = norm1 / norm0
     alpha1 = norm1 / (curve1 - beta * norm1 / alpha0)
@@ -1086,15 +1115,18 @@
     sem = pltpu.SemaphoreType.DMA
     wide = lat_cells
     reach = lon_cells + 2 * 16 * pl.cdiv(BAND, 16)
-    copies = 9 + 2 * (2 + 2 + half + 2 + 1) + 2 * (group - 1 + lat_n - 1 + mem_n - 1)
+    copies = 8 + half + 2 * (9 + half) + 2 * (group - 1 + lat_n - 1)
     scratch = [
         v((members, levels, full, wide), BF16),
         v((members, full, 2 * wide), BF16),
         v((members, full, wide), BF16),
         v((members, full, wide), BF16),
-        v((full, wide), F32),
+        v((levels, full, wide), F32),
+        v((levels, reach - lon_cells, wide), F32),
         v((full, 2 * wide), F32),
+        v((reach, 2 * wide), F32),
         v((2, full, wide), F32),
+        v((2, reach, wide), F32),
         v((lon_n, 1, n_obs), jnp.int32),
         v((lon_n, 1, n_obs), F32),
         v((lon_n, 1, n_obs), F32),
@@ -1109,10 +1141,12 @@
         v((2, levels, 4 * wide, 2 * wide), BF16),
         v((levels, 2 * full, 2 * full), BF16),
         v((levels, 2 * lon_cells, 2 * reach), BF16),
-        v((members, full, 4 * wide), BF16),
+        v((half, full, 4 * wide), BF16),
+        v(((half + 1) * reach, 4 * wide), BF16),
+        v((max(half * full, (half + 1) * reach), 2 * wide), BF16),
         v((half, levels, full, wide), F32),
         v((levels, 2 * full, half * wide), BF16),
-        v((levels, 2 * reach, half * wide), BF16),
+        v((levels, 2 * reach, (half + 1) * wide), BF16),
         pltpu.SMEM(band_width.shape, jnp.int32),
         sem((copies,)), sem((copies,)), sem((7,)),
         pltpu.SemaphoreType.REGULAR((max(lon_n + mem_n - 2, lat_n - 1) - 1,)),

time: 43.2 us -> 39.5 us (0.914)
  Pallas kernels: 42.4 us -> 38.6 us
    pallas_call x1, Pallas kernels: 41.3 us -> 37.5 us  [paired_device(): pl.pallas_call(kernel, out_shape=[ens, ens, jax.ShapeDtypeStruct((2, leve...]
where the time goes in v3:
time: 39.5 us; the launch traced here: 39.2 us
  Pallas kernels  38.6 us (98%)
  between operations  0.64 us (2%)
    pallas_call x1, Pallas kernels, paired_device(): pl.pallas_call(kernel, out_shape=[ens, ens, jax.ShapeDtypeStruct((2, leve...  37.5 us
    pallas_call x1, Pallas kernels, paired_device(): pl.pallas_call(combine, out_shape=[ens, static], in_specs=[VMEM] * 4, out...  1.1 us

profile of v3, /device:TPU:0, one launch (start us, length us, event | category | flops | bytes accessed | tf_op | source)
XLA Modules:
  0.0 39.2 jit_solution(3050249893207753470)
XLA Ops:
  0.6 37.5 %shard_map.77 = (f32[8,4,64,128]{3,2,1,0:T(8,128)S(1)}, f32[8,4,64,128]{3,2,1,0:T(8,128)S(1)}, f32[2,4,64,128]{3,2,1,0:T(8,128)S(1)}, f32[2,128]{1,0:T(2,128)S(1)}) custom-call(bf16[8,4,64,128]{3,2,1,0:T(8,128)(2,1)} %a_hbm.1, f32[4,64,128]{2,1,0:T(8,128)} %s_hbm.1, s32[1,2048]{1,0:T(1,128)} %bitcast.3, f32[1,2048]{1,0:T(1,128)} %bitcast.4, ...), custom_call_target="tpu_custom_call" | custom-call | tf_op jit(solution)/shard_map/pallas_call | solution.py:1158
  38.1 1.1 %shard_map.78 = (f32[8,4,64,128]{3,2,1,0:T(8,128)}, f32[4,64,128]{2,1,0:T(8,128)}) custom-call(f32[8,4,64,128]{3,2,1,0:T(8,128)S(1)} %get-tuple-element.6.ub_ref, f32[8,4,64,128]{3,2,1,0:T(8,128)S(1)} %get-tuple-element.7.uq_ref, f32[2,4,64,128]{3,2,1,0:T(8,128)S(1)} %get-tuple-element.8.st_ref, f32[2,128]{1,0:T(2,128)S(1)} %get-tuple-element.9.coef_ref), custom_call_target="tpu_custom_call" | custom-call | tf_op jit(solution)/shard_map/pallas_call | solution.py:1178

commit v4 on v3

--- a/solution.py
+++ b/solution.py
@@ -1060,13 +1060,11 @@
         return 0
 
     lax.fori_loop(0, levels, center_all, 0)
-    for copy in (lat_a3, lat_a4, lat_s3, lat_s4):
-        copy.wait()
-    out_second(0)
-
     lat_q.wait()
     sharing = rim_and_cov(1)
     out_first(1)
+    for copy in (lat_a3, lat_a4, lat_s3, lat_s4):
+        copy.wait()
     out_second(1)
 
     cq = shared(sharing, 1)
@@ -1079,6 +1077,7 @@
         [resid[s] * cr[s] for s in range(lon_n)],
         [cr[s] * (resid[s] + ow[s] * cr[s]) for s in range(lon_n)],
     )
+    out_second(0)
     norm1, curve1 = dots_end(dots1, 1)
     beta = norm1 / norm0
     alpha1 = norm1 / (curve1 - beta * norm1 / alpha0)

time: 39.5 us -> 38.5 us (0.975)
  Pallas kernels: 38.6 us -> 37.7 us
    pallas_call x1, Pallas kernels: 37.5 us -> 36.6 us  [paired_device(): pl.pallas_call(kernel, out_shape=[ens, ens, jax.ShapeDtypeStruct((2, leve...]
where the time goes in v4:
time: 38.5 us; the launch traced here: 38.3 us
  Pallas kernels  37.7 us (98%)
  between operations  0.64 us (2%)
    pallas_call x1, Pallas kernels, paired_device(): pl.pallas_call(kernel, out_shape=[ens, ens, jax.ShapeDtypeStruct((2, leve...  36.6 us
    pallas_call x1, Pallas kernels, paired_device(): pl.pallas_call(combine, out_shape=[ens, static], in_specs=[VMEM] * 4, out...  1.1 us

profile of v4, /device:TPU:0, one launch (start us, length us, event | category | flops | bytes accessed | tf_op | source)
XLA Modules:
  0.0 38.3 jit_solution(2742167277667695501)
XLA Ops:
  0.6 36.6 %shard_map.77 = (f32[8,4,64,128]{3,2,1,0:T(8,128)S(1)}, f32[8,4,64,128]{3,2,1,0:T(8,128)S(1)}, f32[2,4,64,128]{3,2,1,0:T(8,128)S(1)}, f32[2,128]{1,0:T(2,128)S(1)}) custom-call(bf16[8,4,64,128]{3,2,1,0:T(8,128)(2,1)} %a_hbm.1, f32[4,64,128]{2,1,0:T(8,128)} %s_hbm.1, s32[1,2048]{1,0:T(1,128)} %bitcast.3, f32[1,2048]{1,0:T(1,128)} %bitcast.4, ...), custom_call_target="tpu_custom_call" | custom-call | tf_op jit(solution)/shard_map/pallas_call | solution.py:1157
  37.2 1.1 %shard_map.78 = (f32[8,4,64,128]{3,2,1,0:T(8,128)}, f32[4,64,128]{2,1,0:T(8,128)}) custom-call(f32[8,4,64,128]{3,2,1,0:T(8,128)S(1)} %get-tuple-element.6.ub_ref, f32[8,4,64,128]{3,2,1,0:T(8,128)S(1)} %get-tuple-element.7.uq_ref, f32[2,4,64,128]{3,2,1,0:T(8,128)S(1)} %get-tuple-element.8.st_ref, f32[2,128]{1,0:T(2,128)S(1)} %get-tuple-element.9.coef_ref), custom_call_target="tpu_custom_call" | custom-call | tf_op jit(solution)/shard_map/pallas_call | solution.py:1177

commit v5 on v3

--- a/solution.py
+++ b/solution.py
@@ -957,7 +957,7 @@
 
         lax.fori_loop(0, levels, go, 0)
 
-    def out_second(g):
+    def out_second(g, start, stop):
         out_ref = (ub_ref, uq_ref)[g]
         near_rim = reached(grim[g])
         for p in range(half):
@@ -973,7 +973,7 @@
             st_ref[g, l] = us[half] * coef_static
             return 0
 
-        lax.fori_loop(0, levels, go, 0)
+        lax.fori_loop(start, stop, go, 0)
 
     def dots_start(g, left, right):
         def total(pairs):
@@ -1016,11 +1016,11 @@
                 for p in range(half):
                     part = tc[p, l] + t[p * full : (p + 1) * full]
                     ts[l, :, p * wide : (p + 1) * wide] = stack(part)
-        for l in range(levels):
-            cov_level(l)
         if g == 0:
             lat_s.wait()
             lat_s2.wait()
+        for l in range(levels):
+            cov_level(l)
         cov_static(g)
         return share(g)
 
@@ -1028,6 +1028,7 @@
     lat_a.wait()
     sharing = rim_and_cov(0)
 
+    out_first(0)
     for copy in x_edge:
         copy.wait()
 
@@ -1041,7 +1042,6 @@
     pack_statics(sedge, slice(None), edges, 2 * edge)
     lat_s4 = lat_static(edges, spacks, srims)
     lat_s4.start()
-    out_first(0)
 
     cz = shared(sharing, 0)
     z = [ow[s] * ov[s] for s in range(lon_n)]
@@ -1062,12 +1062,11 @@
     lax.fori_loop(0, levels, center_all, 0)
     for copy in (lat_a3, lat_a4, lat_s3, lat_s4):
         copy.wait()
-    out_second(0)
-
+    out_second(0, 0, levels // 2)
     lat_q.wait()
     sharing = rim_and_cov(1)
     out_first(1)
-    out_second(1)
+    out_second(1, 0, levels - 1)
 
     cq = shared(sharing, 1)
     norm0, curve0 = dots_end(dots0, 0)
@@ -1079,6 +1078,8 @@
         [resid[s] * cr[s] for s in range(lon_n)],
         [cr[s] * (resid[s] + ow[s] * cr[s]) for s in range(lon_n)],
     )
+    out_second(0, levels // 2, levels)
+    out_second(1, levels - 1, levels)
     norm1, curve1 = dots_end(dots1, 1)
     beta = norm1 / norm0
     alpha1 = norm1 / (curve1 - beta * norm1 / alpha0)

time: 39.5 us -> 37.9 us (0.959)
  Pallas kernels: 38.6 us -> 37 us
    pallas_call x1, Pallas kernels: 37.5 us -> 35.9 us  [paired_device(): pl.pallas_call(kernel, out_shape=[ens, ens, jax.ShapeDtypeStruct((2, leve...]
where the time goes in v5:
time: 37.9 us; the launch traced here: 37.7 us
  Pallas kernels  37 us (98%)
  between operations  0.64 us (2%)
    pallas_call x1, Pallas kernels, paired_device(): pl.pallas_call(kernel, out_shape=[ens, ens, jax.ShapeDtypeStruct((2, leve...  35.9 us
    pallas_call x1, Pallas kernels, paired_device(): pl.pallas_call(combine, out_shape=[ens, static], in_specs=[VMEM] * 4, out...  1.1 us

profile of v5, /device:TPU:0, one launch (start us, length us, event | category | flops | bytes accessed | tf_op | source)
XLA Modules:
  0.0 37.7 jit_solution(13836980582894264817)
XLA Ops:
  0.6 35.9 %shard_map.77 = (f32[8,4,64,128]{3,2,1,0:T(8,128)S(1)}, f32[8,4,64,128]{3,2,1,0:T(8,128)S(1)}, f32[2,4,64,128]{3,2,1,0:T(8,128)S(1)}, f32[2,128]{1,0:T(2,128)S(1)}) custom-call(bf16[8,4,64,128]{3,2,1,0:T(8,128)(2,1)} %a_hbm.1, f32[4,64,128]{2,1,0:T(8,128)} %s_hbm.1, s32[1,2048]{1,0:T(1,128)} %bitcast.3, f32[1,2048]{1,0:T(1,128)} %bitcast.4, ...), custom_call_target="tpu_custom_call" | custom-call | tf_op jit(solution)/shard_map/pallas_call | solution.py:1159
  36.6 1.1 %shard_map.78 = (f32[8,4,64,128]{3,2,1,0:T(8,128)}, f32[4,64,128]{2,1,0:T(8,128)}) custom-call(f32[8,4,64,128]{3,2,1,0:T(8,128)S(1)} %get-tuple-element.6.ub_ref, f32[8,4,64,128]{3,2,1,0:T(8,128)S(1)} %get-tuple-element.7.uq_ref, f32[2,4,64,128]{3,2,1,0:T(8,128)S(1)} %get-tuple-element.8.st_ref, f32[2,128]{1,0:T(2,128)S(1)} %get-tuple-element.9.coef_ref), custom_call_target="tpu_custom_call" | custom-call | tf_op jit(solution)/shard_map/pallas_call | solution.py:1179
